TPU v7x, 8 devices: a whole 2x2x1 slice. The times are simulated.
8 devices in a mesh: dp: 1 (over z), cp: 8 (over y, x, core).
Axes of the slice: x: 2, y: 2, z: 1, core: 2. Of those that a mesh axis runs over, the one named last changes fastest.
Arguments:
- x_in: bfloat16 [512, 3584], P(('dp', 'cp'))
- cache_k1: bfloat16 [16384, 4, 128], P(('dp', 'cp'))
- cache_v1: bfloat16 [16384, 4, 128], P(('dp', 'cp'))
- w_q1: bfloat16 [3584, 3584], replicated
- b_q1: bfloat16 [3584], replicated
- w_k1: bfloat16 [3584, 512], replicated
- b_k1: bfloat16 [512], replicated
- w_v1: bfloat16 [3584, 512], replicated
- w_o1: bfloat16 [3584, 3584], replicated
- w_gate: bfloat16 [3584, 18944], replicated
- w_up: bfloat16 [3584, 18944], replicated
- w_down: bfloat16 [18944, 3584], replicated
- cache_k2: bfloat16 [16384, 4, 128], P(('dp', 'cp'))
- cache_v2: bfloat16 [16384, 4, 128], P(('dp', 'cp'))
- w_q2: bfloat16 [3584, 3584], replicated
- b_q2: bfloat16 [3584], replicated
- w_k2: bfloat16 [3584, 512], replicated
- b_k2: bfloat16 [512], replicated
- w_v2: bfloat16 [3584, 512], replicated
- w_o2: bfloat16 [3584, 3584], replicated
Outputs:
- output 1: bfloat16 [512, 3584], P(('dp', 'cp'))
- output 2: bfloat16 [512, 3584], P(('dp', 'cp'))
- output 3: bfloat16 [512, 4, 128], P(('dp', 'cp'))
- output 4: bfloat16 [512, 4, 128], P(('dp', 'cp'))
- output 5: bfloat16 [512, 4, 128], P(('dp', 'cp'))
- output 6: bfloat16 [512, 4, 128], P(('dp', 'cp'))
All inputs are finite; a program needn't handle non-finite values.
Results may differ from a plain program's by a relative error of at most 0.0144252.
Values are sent between devices in bfloat16 or wider.
A program may use at most 2 GiB of HBM per device.

v0:
```python
import jax
import jax.numpy as jnp
from jax import lax
from jax.sharding import PartitionSpec as P

ROPE_THETA = 500000.0
NORM_EPS = 1e-5


def rms_norm(vals):
    wide = vals.astype(jnp.float32)
    return (wide * lax.rsqrt(jnp.mean(wide * wide, axis=-1, keepdims=True) + NORM_EPS)).astype(jnp.bfloat16)


def rope_tables(positions, head_dim):
    half_dim = head_dim // 2
    inv_freq = 1.0 / (ROPE_THETA ** (jnp.arange(half_dim, dtype=jnp.float32) * (2.0 / head_dim)))
    angles = positions.astype(jnp.float32)[:, None] * inv_freq[None, :]
    return jnp.cos(angles)[:, None, :], jnp.sin(angles)[:, None, :]


def apply_rope(vals, cos_t, sin_t):
    half_dim = vals.shape[-1] // 2
    first = vals[..., :half_dim]
    second = vals[..., half_dim:]
    return jnp.concatenate([first * cos_t - second * sin_t, second * cos_t + first * sin_t], axis=-1)


def project_rows(layer_in, w_q, b_q, w_k, b_k, w_v, positions, head_dim):
    rows = layer_in.shape[0]
    cos_t, sin_t = rope_tables(positions, head_dim)
    q_pre = (jnp.dot(layer_in, w_q, preferred_element_type=jnp.float32) + b_q.astype(jnp.float32)).astype(jnp.bfloat16)
    k_pre = (jnp.dot(layer_in, w_k, preferred_element_type=jnp.float32) + b_k.astype(jnp.float32)).astype(jnp.bfloat16)
    v_new = jnp.dot(layer_in, w_v, preferred_element_type=jnp.float32).astype(jnp.bfloat16).reshape(rows, -1, head_dim)
    q_rot = apply_rope(q_pre.reshape(rows, -1, head_dim).astype(jnp.float32), cos_t, sin_t).astype(jnp.bfloat16)
    k_new = apply_rope(k_pre.reshape(rows, -1, head_dim).astype(jnp.float32), cos_t, sin_t).astype(jnp.bfloat16)
    return q_rot, k_new, v_new


def mlp_block(resid_h, w_gate, w_up, w_down):
    normed = rms_norm(resid_h)
    gate_act = jnp.dot(normed, w_gate, preferred_element_type=jnp.float32).astype(jnp.bfloat16)
    up_proj = jnp.dot(normed, w_up, preferred_element_type=jnp.float32).astype(jnp.bfloat16)
    mixed = (jax.nn.silu(gate_act.astype(jnp.float32)) * up_proj.astype(jnp.float32)).astype(jnp.bfloat16)
    return (resid_h.astype(jnp.float32) + jnp.dot(mixed, w_down, preferred_element_type=jnp.float32)).astype(jnp.bfloat16)


def partial_attend(q_grp, keys, values, scale, visible):
    scores = jnp.einsum('tkgd,skd->tkgs', q_grp, keys, preferred_element_type=jnp.float32) * scale
    if visible is not None:
        scores = jnp.where(visible, scores, -jnp.inf)
    peak = jnp.max(scores, axis=-1)
    prob_w = jnp.exp(scores - peak[..., None])
    total = jnp.sum(prob_w, axis=-1)
    summed = jnp.einsum('tkgs,skd->tkgd', prob_w.astype(jnp.bfloat16), values, preferred_element_type=jnp.float32)
    return summed / total[..., None], peak + jnp.log(total)


def merge_parts(out_a, lse_a, out_b, lse_b):
    lse_new = jnp.logaddexp(lse_a, lse_b)
    merged = out_a * jnp.exp(lse_a - lse_new)[..., None] + out_b * jnp.exp(lse_b - lse_new)[..., None]
    return merged, lse_new


def attention_layer(layer_in, cache_k, cache_v, w_q, b_q, w_k, b_k, w_v, w_o, axis_size):
    tok_dev = layer_in.shape[0]
    cache_dev, kv_heads, head_dim = cache_k.shape
    heads = w_q.shape[1] // head_dim
    my_idx = lax.axis_index('cp')
    positions = axis_size * cache_dev + my_idx * tok_dev + jnp.arange(tok_dev)
    q_rot, k_new, v_new = project_rows(layer_in, w_q, b_q, w_k, b_k, w_v, positions, head_dim)
    q_grp = q_rot.reshape(tok_dev, kv_heads, heads // kv_heads, head_dim)
    scale = head_dim ** -0.5
    all_k = lax.all_gather(k_new, 'cp', axis=0, tiled=True)
    all_v = lax.all_gather(v_new, 'cp', axis=0, tiled=True)
    q_pos = my_idx * tok_dev + jnp.arange(tok_dev)
    visible = (jnp.arange(axis_size * tok_dev)[None, :] <= q_pos[:, None])[:, None, None, :]
    out_acc, lse_acc = partial_attend(q_grp, all_k, all_v, scale, visible)
    out_loc, lse_loc = partial_attend(q_grp, cache_k, cache_v, scale, None)
    out_acc, lse_acc = merge_parts(out_acc, lse_acc, out_loc, lse_loc)
    shift = [(src_idx, (src_idx + 1) % axis_size) for src_idx in range(axis_size)]

    def cache_step(step, carry):
        blk_k, blk_v, out_run, lse_run = carry
        blk_k = lax.ppermute(blk_k, 'cp', shift)
        blk_v = lax.ppermute(blk_v, 'cp', shift)
        out_blk, lse_blk = partial_attend(q_grp, blk_k, blk_v, scale, None)
        out_run, lse_run = merge_parts(out_run, lse_run, out_blk, lse_blk)
        return blk_k, blk_v, out_run, lse_run

    carry_end = lax.fori_loop(0, axis_size - 1, cache_step, (cache_k, cache_v, out_acc, lse_acc))
    o_half = carry_end[2].astype(jnp.bfloat16).reshape(tok_dev, heads * head_dim)
    y_out = jnp.dot(o_half, w_o, preferred_element_type=jnp.float32).astype(jnp.bfloat16)
    return y_out, k_new, v_new


def solution(mesh):
    axis_size = mesh.shape['cp']
    rows_spec = P(('dp', 'cp'), None)
    cache_spec = P(('dp', 'cp'), None, None)
    mat_spec = P(None, None)
    vec_spec = P(None)
    layer_specs = (cache_spec, cache_spec, mat_spec, vec_spec, mat_spec, vec_spec, mat_spec, mat_spec)
    in_specs = (rows_spec,) + layer_specs + (mat_spec, mat_spec, mat_spec) + layer_specs
    out_specs = (rows_spec, rows_spec, cache_spec, cache_spec, cache_spec, cache_spec)

    def forward(x_in, cache_k1, cache_v1, w_q1, b_q1, w_k1, b_k1, w_v1, w_o1, w_gate, w_up, w_down, cache_k2, cache_v2, w_q2, b_q2, w_k2, b_k2, w_v2, w_o2):
        y_one, k_one, v_one = attention_layer(x_in, cache_k1, cache_v1, w_q1, b_q1, w_k1, b_k1, w_v1, w_o1, axis_size)
        resid_h = (x_in.astype(jnp.float32) + y_one.astype(jnp.float32)).astype(jnp.bfloat16)
        hidden = mlp_block(resid_h, w_gate, w_up, w_down)
        y_two, k_two, v_two = attention_layer(rms_norm(hidden), cache_k2, cache_v2, w_q2, b_q2, w_k2, b_k2, w_v2, w_o2, axis_size)
        return hidden, y_two, k_one, v_one, k_two, v_two

    return jax.shard_map(forward, mesh=mesh, in_specs=in_specs, out_specs=out_specs, check_vma=False)
```

profile of v0, /device:TPU:0, one launch (start us, length us, event | category | flops | bytes accessed | tf_op | source)
XLA Modules:
  0.0 1155.8 jit_solution(14712073393701376574)
XLA Ops:
  4.9 15.4 %all_gather.13 = bf16[512,4,128]{2,0,1:T(8,128)(2,1)S(1)} all-gather(bf16[64,4,128]{2,0,1:T(8,128)(2,1)S(1)} %pad_maximum_fusion.2), channel_id=1, replica_groups=mesh['dp'=1,'cp'=8] {'cp'}, dimensions={0}, use_global_device_ids=true | all-gather | bytes 589824 | tf_op jit(solution)/shard_map/all_gather | solution.py:74
  20.3 10.7 fusion.89
  41.7 7.7 fusion.69
  49.5 8.6 fusion.174
  59.5 12.6 %all_gather.12 = bf16[512,4,128]{2,0,1:T(8,128)(2,1)S(1)} all-gather(bf16[64,4,128]{2,0,1:T(8,128)(2,1)S(1)} %copy_bitcast_fusion.1), channel_id=1, replica_groups=mesh['dp'=1,'cp'=8] {'cp'}, dimensions={0}, use_global_device_ids=true | all-gather | bytes 589824 | tf_op jit(solution)/shard_map/all_gather | solution.py:75
  78.1 422.0 %while.32 = (s32[]{:T(128)}, bf16[2048,4,128]{2,0,1:T(8,128)(2,1)}, bf16[2048,4,128]{2,0,1:T(8,128)(2,1)}, f32[64,4,7,128]{3,0,2,1:T(8,128)}, f32[64,4,7]{0,2,1:...) while((s32[]{:T(128)}, bf16[2048,4,128]{2,0,1:T(8,128)(2,1)}, bf16[2048,4,128]{2,0,1:T(8,128)(2,1)}, ...), condition=%wide.region_7.8_spmd, body=%wide.region_4.7_spmd.sunk | while | flops 1909343744 | bytes 83149016 | solution.py:91
  78.6 25.9 %collective-permute-done = bf16[2048,4,128]{2,0,1:T(8,128)(2,1)S(1)} collective-permute-done((bf16[2048,4,128]{2,0,1:T(8,128)(2,1)}, bf16[2048,4,128]{2,0,1:T(8,128)(2,1)S(1)}, u32[]{:S(2)}, u32[]{:S(2)}) %collective-permute-start) | collective-permute-done | bytes 2097184 | tf_op jit(solution)/shard_map/while/body/eval_jaxpr/ppermute | solution.py:85
  113.0 7.7 fusion.245
  138.4 26.4 %collective-permute-done = bf16[2048,4,128]{2,0,1:T(8,128)(2,1)S(1)} collective-permute-done((bf16[2048,4,128]{2,0,1:T(8,128)(2,1)}, bf16[2048,4,128]{2,0,1:T(8,128)(2,1)S(1)}, u32[]{:S(2)}, u32[]{:S(2)}) %collective-permute-start) | collective-permute-done | bytes 2097184 | tf_op jit(solution)/shard_map/while/body/eval_jaxpr/ppermute | solution.py:85
  173.3 7.7 fusion.245
  198.7 26.4 %collective-permute-done = bf16[2048,4,128]{2,0,1:T(8,128)(2,1)S(1)} collective-permute-done((bf16[2048,4,128]{2,0,1:T(8,128)(2,1)}, bf16[2048,4,128]{2,0,1:T(8,128)(2,1)S(1)}, u32[]{:S(2)}, u32[]{:S(2)}) %collective-permute-start) | collective-permute-done | bytes 2097184 | tf_op jit(solution)/shard_map/while/body/eval_jaxpr/ppermute | solution.py:85
  233.6 7.7 fusion.245
  259.0 26.4 %collective-permute-done = bf16[2048,4,128]{2,0,1:T(8,128)(2,1)S(1)} collective-permute-done((bf16[2048,4,128]{2,0,1:T(8,128)(2,1)}, bf16[2048,4,128]{2,0,1:T(8,128)(2,1)S(1)}, u32[]{:S(2)}, u32[]{:S(2)}) %collective-permute-start) | collective-permute-done | bytes 2097184 | tf_op jit(solution)/shard_map/while/body/eval_jaxpr/ppermute | solution.py:85
  293.9 7.7 fusion.245
  319.2 26.4 %collective-permute-done = bf16[2048,4,128]{2,0,1:T(8,128)(2,1)S(1)} collective-permute-done((bf16[2048,4,128]{2,0,1:T(8,128)(2,1)}, bf16[2048,4,128]{2,0,1:T(8,128)(2,1)S(1)}, u32[]{:S(2)}, u32[]{:S(2)}) %collective-permute-start) | collective-permute-done | bytes 2097184 | tf_op jit(solution)/shard_map/while/body/eval_jaxpr/ppermute | solution.py:85
  354.2 7.7 fusion.245
  379.5 26.4 %collective-permute-done = bf16[2048,4,128]{2,0,1:T(8,128)(2,1)S(1)} collective-permute-done((bf16[2048,4,128]{2,0,1:T(8,128)(2,1)}, bf16[2048,4,128]{2,0,1:T(8,128)(2,1)S(1)}, u32[]{:S(2)}, u32[]{:S(2)}) %collective-permute-start) | collective-permute-done | bytes 2097184 | tf_op jit(solution)/shard_map/while/body/eval_jaxpr/ppermute | solution.py:85
  414.5 7.7 fusion.245
  439.8 26.4 %collective-permute-done = bf16[2048,4,128]{2,0,1:T(8,128)(2,1)S(1)} collective-permute-done((bf16[2048,4,128]{2,0,1:T(8,128)(2,1)}, bf16[2048,4,128]{2,0,1:T(8,128)(2,1)S(1)}, u32[]{:S(2)}, u32[]{:S(2)}) %collective-permute-start) | collective-permute-done | bytes 2097184 | tf_op jit(solution)/shard_map/while/body/eval_jaxpr/ppermute | solution.py:85
  474.8 7.7 fusion.245
  502.2 10.8 multiply_reduce_fusion
  513.0 46.7 %fusion.64 = f32[64,18944]{1,0:T(8,128)} fusion(bf16[3584,18944]{1,0:T(8,128)(2,1)} %param.33, f32[64,3584]{1,0:T(8,128)S(1)} %get-tuple-element.163, f32[64]{0:T(128)S(1)} %add_rsqrt_fusion.1), kind=kOutput, calls=%fused_computation.44 | convolution fusion | flops 8693481472 | bytes 141558016 | tf_op jit(solution)/shard_map/dot_general | solution.py:42
  559.7 46.9 %fusion.65.clone.5.clone.4 = bf16[64,18944]{1,0:T(8,128)(2,1)S(1)} fusion(bf16[3584,18944]{1,0:T(8,128)(2,1)} %param.34, f32[64,18944]{1,0:T(8,128)} %fusion.64, f32[64,3584]{1,0:T(8,128)S(1)} %get-tuple-element.163, f32[64]{0:T(128)S(1)} %add_rsqrt_fusion.1), kind=kOutput, calls=%fused_computation.45.clone.clone.clone.clone.clone.clone.clone.clone.clone.1 | convolution fusion | flops 8700755968 | bytes 143982848 | tf_op jit(solution)/shard_map/dot_general | solution.py:43
  606.6 45.7 %fusion.179 = (f32[64]{0:T(128)S(1)}, bf16[64,3584]{1,0:T(8,128)(2,1)}) fusion(f32[64,3584]{1,0:T(8,128)S(1)} %get-tuple-element.163, bf16[18944,3584]{1,0:T(8,128)(2,1)} %param.35, bf16[64,18944]{1,0:T(8,128)(2,1)S(1)} %fusion.65.clone.5.clone.4), kind=kOutput, calls=%fused_computation.137 | convolution fusion | flops 8691744768 | bytes 139591936 | tf_op jit(solution)/shard_map/dot_general | solution.py:45
  655.4 12.6 %all_gather.14 = bf16[512,4,128]{2,0,1:T(8,128)(2,1)} all-gather(bf16[64,4,128]{2,0,1:T(8,128)(2,1)S(1)} %copy_bitcast_fusion), channel_id=1, replica_groups=mesh['dp'=1,'cp'=8] {'cp'}, dimensions={0}, use_global_device_ids=true | all-gather | bytes 589824 | tf_op jit(solution)/shard_map/all_gather | solution.py:75
  668.1 10.9 fusion.91
  688.1 7.9 fusion.71
  697.2 12.6 %all_gather.15 = bf16[512,4,128]{2,0,1:T(8,128)(2,1)S(1)} all-gather(bf16[64,4,128]{2,0,1:T(8,128)(2,1)S(1)} %pad_maximum_fusion.3), channel_id=1, replica_groups=mesh['dp'=1,'cp'=8] {'cp'}, dimensions={0}, use_global_device_ids=true | all-gather | bytes 589824 | tf_op jit(solution)/shard_map/all_gather | solution.py:74
  724.3 415.9 %while.33 = (s32[]{:T(128)}, bf16[2048,4,128]{2,0,1:T(8,128)(2,1)}, bf16[2048,4,128]{2,0,1:T(8,128)(2,1)}, f32[64,4,7,128]{3,0,2,1:T(8,128)S(1)}, f32[64,4,7]{0,...) while((s32[]{:T(128)}, bf16[2048,4,128]{2,0,1:T(8,128)(2,1)}, ...), condition=%wide.region_17.18_spmd, body=%wide.region_14.17_spmd.sunk | while | flops 1909343744 | bytes 75808928 | solution.py:91
  725.1 25.6 %collective-permute-done.2 = bf16[2048,4,128]{2,0,1:T(8,128)(2,1)S(1)} collective-permute-done((bf16[2048,4,128]{2,0,1:T(8,128)(2,1)}, bf16[2048,4,128]{2,0,1:T(8,128)(2,1)S(1)}, u32[]{:S(2)}, u32[]{:S(2)}) %collective-permute-start.2) | collective-permute-done | bytes 2097184 | tf_op jit(solution)/shard_map/while/body/eval_jaxpr/ppermute | solution.py:85
  759.3 7.7 fusion.250
  776.2 7.5 fusion.251
  783.8 26.3 %collective-permute-done.2 = bf16[2048,4,128]{2,0,1:T(8,128)(2,1)S(1)} collective-permute-done((bf16[2048,4,128]{2,0,1:T(8,128)(2,1)}, bf16[2048,4,128]{2,0,1:T(8,128)(2,1)S(1)}, u32[]{:S(2)}, u32[]{:S(2)}) %collective-permute-start.2) | collective-permute-done | bytes 2097184 | tf_op jit(solution)/shard_map/while/body/eval_jaxpr/ppermute | solution.py:85
  818.7 7.7 fusion.250
  835.6 7.5 fusion.251
  843.2 26.3 %collective-permute-done.2 = bf16[2048,4,128]{2,0,1:T(8,128)(2,1)S(1)} collective-permute-done((bf16[2048,4,128]{2,0,1:T(8,128)(2,1)}, bf16[2048,4,128]{2,0,1:T(8,128)(2,1)S(1)}, u32[]{:S(2)}, u32[]{:S(2)}) %collective-permute-start.2) | collective-permute-done | bytes 2097184 | tf_op jit(solution)/shard_map/while/body/eval_jaxpr/ppermute | solution.py:85
  878.2 7.7 fusion.250
  895.1 7.5 fusion.251
  902.7 26.3 %collective-permute-done.2 = bf16[2048,4,128]{2,0,1:T(8,128)(2,1)S(1)} collective-permute-done((bf16[2048,4,128]{2,0,1:T(8,128)(2,1)}, bf16[2048,4,128]{2,0,1:T(8,128)(2,1)S(1)}, u32[]{:S(2)}, u32[]{:S(2)}) %collective-permute-start.2) | collective-permute-done | bytes 2097184 | tf_op jit(solution)/shard_map/while/body/eval_jaxpr/ppermute | solution.py:85
  937.6 7.7 fusion.250
  962.1 26.3 %collective-permute-done.2 = bf16[2048,4,128]{2,0,1:T(8,128)(2,1)S(1)} collective-permute-done((bf16[2048,4,128]{2,0,1:T(8,128)(2,1)}, bf16[2048,4,128]{2,0,1:T(8,128)(2,1)S(1)}, u32[]{:S(2)}, u32[]{:S(2)}) %collective-permute-start.2) | collective-permute-done | bytes 2097184 | tf_op jit(solution)/shard_map/while/body/eval_jaxpr/ppermute | solution.py:85
  997.0 7.7 fusion.250
  1021.5 26.3 %collective-permute-done.2 = bf16[2048,4,128]{2,0,1:T(8,128)(2,1)S(1)} collective-permute-done((bf16[2048,4,128]{2,0,1:T(8,128)(2,1)}, bf16[2048,4,128]{2,0,1:T(8,128)(2,1)S(1)}, u32[]{:S(2)}, u32[]{:S(2)}) %collective-permute-start.2) | collective-permute-done | bytes 2097184 | tf_op jit(solution)/shard_map/while/body/eval_jaxpr/ppermute | solution.py:85
  1056.4 7.7 fusion.250
  1073.3 7.5 fusion.251
  1080.9 26.3 %collective-permute-done.2 = bf16[2048,4,128]{2,0,1:T(8,128)(2,1)S(1)} collective-permute-done((bf16[2048,4,128]{2,0,1:T(8,128)(2,1)}, bf16[2048,4,128]{2,0,1:T(8,128)(2,1)S(1)}, u32[]{:S(2)}, u32[]{:S(2)}) %collective-permute-start.2) | collective-permute-done | bytes 2097184 | tf_op jit(solution)/shard_map/while/body/eval_jaxpr/ppermute | solution.py:85
  1115.8 7.7 fusion.250
  1141.2 11.5 convolution_convert_fusion.2
  (262 shorter events, 387.5 us)
Async XLA Ops:
  0.6 19.7 %copy-start.3 = (bf16[64,3584]{1,0:T(8,128)(2,1)S(1)}, bf16[64,3584]{1,0:T(8,128)(2,1)}, u32[]{:S(2)}) copy-start(bf16[64,3584]{1,0:T(8,128)(2,1)} %param.24) | copy-start | bytes 1376260
  0.6 19.6 %copy-start.24 = (bf16[3584]{0:T(1024)(128)(2,1)S(1)}, bf16[3584]{0:T(1024)(128)(2,1)}, u32[]{:S(2)}) copy-start(bf16[3584]{0:T(1024)(128)(2,1)} %param.28) | copy-start | bytes 21508
  0.9 30.3 %copy-start.13 = (f32[64,64]{1,0:T(8,128)}, f32[64,64]{1,0:T(8,128)S(1)}, u32[]{:S(2)}) copy-start(f32[64,64]{1,0:T(8,128)S(1)} %get-tuple-element.156) | copy-start | bytes 49156
  0.9 30.3 %copy-start.15 = (f32[64,64]{1,0:T(8,128)}, f32[64,64]{1,0:T(8,128)S(1)}, u32[]{:S(2)}) copy-start(f32[64,64]{1,0:T(8,128)S(1)} %get-tuple-element.157) | copy-start | bytes 49156
  4.9 26.1 %copy-start.19 = (bf16[64,4,128]{2,0,1:T(8,128)(2,1)}, bf16[64,4,128]{2,0,1:T(8,128)(2,1)S(1)}, u32[]{:S(2)}) copy-start(bf16[64,4,128]{2,0,1:T(8,128)(2,1)S(1)} %pad_maximum_fusion.2) | copy-start | bytes 196612
  32.5 39.6 %copy-start.11 = (pred[64,512]{1,0:T(8,128)(4,1)}, pred[64,512]{1,0:T(8,128)(4,1)S(1)}, u32[]{:S(2)}) copy-start(pred[64,512]{1,0:T(8,128)(4,1)S(1)} %iota_compare_fusion) | copy-start | bytes 98308
  78.1 26.4 %collective-permute-start = (bf16[2048,4,128]{2,0,1:T(8,128)(2,1)}, bf16[2048,4,128]{2,0,1:T(8,128)(2,1)S(1)}, u32[]{:S(2)}, u32[]{:S(2)}) collective-permute-start(bf16[2048,4,128]{2,0,1:T(8,128)(2,1)} %get-tuple-element.268), channel_id=1, source_target_pairs={{0,1},{1,2},{2,3},{3,4},{4,5},{5,6},{6,7},{7,0}} | collective-permute-start | bytes 6291464 | tf_op jit(solution)/shard_map/while/body/eval_jaxpr/ppermute | solution.py:85
  78.1 48.8 %collective-permute-start.1 = (bf16[2048,4,128]{2,0,1:T(8,128)(2,1)}, bf16[2048,4,128]{2,0,1:T(8,128)(2,1)}, u32[]{:S(2)}, u32[]{:S(2)}) collective-permute-start(bf16[2048,4,128]{2,0,1:T(8,128)(2,1)} %get-tuple-element.269), channel_id=1, source_target_pairs={{0,1},{1,2},{2,3},{3,4},{4,5},{5,6},{6,7},{7,0}} | collective-permute-start | bytes 6291464 | tf_op jit(solution)/shard_map/while/body/eval_jaxpr/ppermute | solution.py:86
  138.4 26.4 %collective-permute-start = (bf16[2048,4,128]{2,0,1:T(8,128)(2,1)}, bf16[2048,4,128]{2,0,1:T(8,128)(2,1)S(1)}, u32[]{:S(2)}, u32[]{:S(2)}) collective-permute-start(bf16[2048,4,128]{2,0,1:T(8,128)(2,1)} %get-tuple-element.268), channel_id=1, source_target_pairs={{0,1},{1,2},{2,3},{3,4},{4,5},{5,6},{6,7},{7,0}} | collective-permute-start | bytes 6291464 | tf_op jit(solution)/shard_map/while/body/eval_jaxpr/ppermute | solution.py:85
  138.4 48.8 %collective-permute-start.1 = (bf16[2048,4,128]{2,0,1:T(8,128)(2,1)}, bf16[2048,4,128]{2,0,1:T(8,128)(2,1)}, u32[]{:S(2)}, u32[]{:S(2)}) collective-permute-start(bf16[2048,4,128]{2,0,1:T(8,128)(2,1)} %get-tuple-element.269), channel_id=1, source_target_pairs={{0,1},{1,2},{2,3},{3,4},{4,5},{5,6},{6,7},{7,0}} | collective-permute-start | bytes 6291464 | tf_op jit(solution)/shard_map/while/body/eval_jaxpr/ppermute | solution.py:86
  181.0 9.2 copy-start.9
  198.7 26.4 %collective-permute-start = (bf16[2048,4,128]{2,0,1:T(8,128)(2,1)}, bf16[2048,4,128]{2,0,1:T(8,128)(2,1)S(1)}, u32[]{:S(2)}, u32[]{:S(2)}) collective-permute-start(bf16[2048,4,128]{2,0,1:T(8,128)(2,1)} %get-tuple-element.268), channel_id=1, source_target_pairs={{0,1},{1,2},{2,3},{3,4},{4,5},{5,6},{6,7},{7,0}} | collective-permute-start | bytes 6291464 | tf_op jit(solution)/shard_map/while/body/eval_jaxpr/ppermute | solution.py:85
  198.7 48.8 %collective-permute-start.1 = (bf16[2048,4,128]{2,0,1:T(8,128)(2,1)}, bf16[2048,4,128]{2,0,1:T(8,128)(2,1)}, u32[]{:S(2)}, u32[]{:S(2)}) collective-permute-start(bf16[2048,4,128]{2,0,1:T(8,128)(2,1)} %get-tuple-element.269), channel_id=1, source_target_pairs={{0,1},{1,2},{2,3},{3,4},{4,5},{5,6},{6,7},{7,0}} | collective-permute-start | bytes 6291464 | tf_op jit(solution)/shard_map/while/body/eval_jaxpr/ppermute | solution.py:86
  241.3 9.2 copy-start.9
  259.0 26.4 %collective-permute-start = (bf16[2048,4,128]{2,0,1:T(8,128)(2,1)}, bf16[2048,4,128]{2,0,1:T(8,128)(2,1)S(1)}, u32[]{:S(2)}, u32[]{:S(2)}) collective-permute-start(bf16[2048,4,128]{2,0,1:T(8,128)(2,1)} %get-tuple-element.268), channel_id=1, source_target_pairs={{0,1},{1,2},{2,3},{3,4},{4,5},{5,6},{6,7},{7,0}} | collective-permute-start | bytes 6291464 | tf_op jit(solution)/shard_map/while/body/eval_jaxpr/ppermute | solution.py:85
  259.0 48.8 %collective-permute-start.1 = (bf16[2048,4,128]{2,0,1:T(8,128)(2,1)}, bf16[2048,4,128]{2,0,1:T(8,128)(2,1)}, u32[]{:S(2)}, u32[]{:S(2)}) collective-permute-start(bf16[2048,4,128]{2,0,1:T(8,128)(2,1)} %get-tuple-element.269), channel_id=1, source_target_pairs={{0,1},{1,2},{2,3},{3,4},{4,5},{5,6},{6,7},{7,0}} | collective-permute-start | bytes 6291464 | tf_op jit(solution)/shard_map/while/body/eval_jaxpr/ppermute | solution.py:86
  301.6 9.2 copy-start.9
  319.2 26.4 %collective-permute-start = (bf16[2048,4,128]{2,0,1:T(8,128)(2,1)}, bf16[2048,4,128]{2,0,1:T(8,128)(2,1)S(1)}, u32[]{:S(2)}, u32[]{:S(2)}) collective-permute-start(bf16[2048,4,128]{2,0,1:T(8,128)(2,1)} %get-tuple-element.268), channel_id=1, source_target_pairs={{0,1},{1,2},{2,3},{3,4},{4,5},{5,6},{6,7},{7,0}} | collective-permute-start | bytes 6291464 | tf_op jit(solution)/shard_map/while/body/eval_jaxpr/ppermute | solution.py:85
  319.2 48.8 %collective-permute-start.1 = (bf16[2048,4,128]{2,0,1:T(8,128)(2,1)}, bf16[2048,4,128]{2,0,1:T(8,128)(2,1)}, u32[]{:S(2)}, u32[]{:S(2)}) collective-permute-start(bf16[2048,4,128]{2,0,1:T(8,128)(2,1)} %get-tuple-element.269), channel_id=1, source_target_pairs={{0,1},{1,2},{2,3},{3,4},{4,5},{5,6},{6,7},{7,0}} | collective-permute-start | bytes 6291464 | tf_op jit(solution)/shard_map/while/body/eval_jaxpr/ppermute | solution.py:86
  379.5 26.4 %collective-permute-start = (bf16[2048,4,128]{2,0,1:T(8,128)(2,1)}, bf16[2048,4,128]{2,0,1:T(8,128)(2,1)S(1)}, u32[]{:S(2)}, u32[]{:S(2)}) collective-permute-start(bf16[2048,4,128]{2,0,1:T(8,128)(2,1)} %get-tuple-element.268), channel_id=1, source_target_pairs={{0,1},{1,2},{2,3},{3,4},{4,5},{5,6},{6,7},{7,0}} | collective-permute-start | bytes 6291464 | tf_op jit(solution)/shard_map/while/body/eval_jaxpr/ppermute | solution.py:85
  379.5 48.8 %collective-permute-start.1 = (bf16[2048,4,128]{2,0,1:T(8,128)(2,1)}, bf16[2048,4,128]{2,0,1:T(8,128)(2,1)}, u32[]{:S(2)}, u32[]{:S(2)}) collective-permute-start(bf16[2048,4,128]{2,0,1:T(8,128)(2,1)} %get-tuple-element.269), channel_id=1, source_target_pairs={{0,1},{1,2},{2,3},{3,4},{4,5},{5,6},{6,7},{7,0}} | collective-permute-start | bytes 6291464 | tf_op jit(solution)/shard_map/while/body/eval_jaxpr/ppermute | solution.py:86
  422.2 9.2 copy-start.9
  439.8 26.4 %collective-permute-start = (bf16[2048,4,128]{2,0,1:T(8,128)(2,1)}, bf16[2048,4,128]{2,0,1:T(8,128)(2,1)S(1)}, u32[]{:S(2)}, u32[]{:S(2)}) collective-permute-start(bf16[2048,4,128]{2,0,1:T(8,128)(2,1)} %get-tuple-element.268), channel_id=1, source_target_pairs={{0,1},{1,2},{2,3},{3,4},{4,5},{5,6},{6,7},{7,0}} | collective-permute-start | bytes 6291464 | tf_op jit(solution)/shard_map/while/body/eval_jaxpr/ppermute | solution.py:85
  439.8 48.8 %collective-permute-start.1 = (bf16[2048,4,128]{2,0,1:T(8,128)(2,1)}, bf16[2048,4,128]{2,0,1:T(8,128)(2,1)}, u32[]{:S(2)}, u32[]{:S(2)}) collective-permute-start(bf16[2048,4,128]{2,0,1:T(8,128)(2,1)} %get-tuple-element.269), channel_id=1, source_target_pairs={{0,1},{1,2},{2,3},{3,4},{4,5},{5,6},{6,7},{7,0}} | collective-permute-start | bytes 6291464 | tf_op jit(solution)/shard_map/while/body/eval_jaxpr/ppermute | solution.py:86
  482.5 9.2 copy-start.9
  652.3 15.7 %copy-start.25 = (bf16[3584]{0:T(1024)(128)(2,1)S(1)}, bf16[3584]{0:T(1024)(128)(2,1)}, u32[]{:S(2)}) copy-start(bf16[3584]{0:T(1024)(128)(2,1)} %param.39) | copy-start | bytes 21508
  652.3 15.7 %copy-start.4 = (bf16[64,3584]{1,0:T(8,128)(2,1)S(1)}, bf16[64,3584]{1,0:T(8,128)(2,1)}, u32[]{:S(2)}) copy-start(bf16[64,3584]{1,0:T(8,128)(2,1)} %get-tuple-element.165) | copy-start | bytes 1376260
  668.0 11.2 copy-start.14
  668.1 11.2 copy-start.16
  696.0 13.7 %copy-start.12 = (pred[64,512]{1,0:T(8,128)(4,1)S(1)}, pred[64,512]{1,0:T(8,128)(4,1)}, u32[]{:S(2)}) copy-start(pred[64,512]{1,0:T(8,128)(4,1)} %copy-done.11) | copy-start | bytes 98308
  697.1 13.3 %copy-start.21 = (bf16[64,4,128]{2,0,1:T(8,128)(2,1)}, bf16[64,4,128]{2,0,1:T(8,128)(2,1)S(1)}, u32[]{:S(2)}) copy-start(bf16[64,4,128]{2,0,1:T(8,128)(2,1)S(1)} %pad_maximum_fusion.3) | copy-start | bytes 196612
  724.4 26.4 %collective-permute-start.2 = (bf16[2048,4,128]{2,0,1:T(8,128)(2,1)}, bf16[2048,4,128]{2,0,1:T(8,128)(2,1)S(1)}, u32[]{:S(2)}, u32[]{:S(2)}) collective-permute-start(bf16[2048,4,128]{2,0,1:T(8,128)(2,1)} %get-tuple-element.289), channel_id=1, source_target_pairs={{0,1},{1,2},{2,3},{3,4},{4,5},{5,6},{6,7},{7,0}} | collective-permute-start | bytes 6291464 | tf_op jit(solution)/shard_map/while/body/eval_jaxpr/ppermute | solution.py:85
  724.4 48.8 %collective-permute-start.3 = (bf16[2048,4,128]{2,0,1:T(8,128)(2,1)}, bf16[2048,4,128]{2,0,1:T(8,128)(2,1)}, u32[]{:S(2)}, u32[]{:S(2)}) collective-permute-start(bf16[2048,4,128]{2,0,1:T(8,128)(2,1)} %get-tuple-element.290), channel_id=1, source_target_pairs={{0,1},{1,2},{2,3},{3,4},{4,5},{5,6},{6,7},{7,0}} | collective-permute-start | bytes 6291464 | tf_op jit(solution)/shard_map/while/body/eval_jaxpr/ppermute | solution.py:86
  783.7 26.4 %collective-permute-start.2 = (bf16[2048,4,128]{2,0,1:T(8,128)(2,1)}, bf16[2048,4,128]{2,0,1:T(8,128)(2,1)S(1)}, u32[]{:S(2)}, u32[]{:S(2)}) collective-permute-start(bf16[2048,4,128]{2,0,1:T(8,128)(2,1)} %get-tuple-element.289), channel_id=1, source_target_pairs={{0,1},{1,2},{2,3},{3,4},{4,5},{5,6},{6,7},{7,0}} | collective-permute-start | bytes 6291464 | tf_op jit(solution)/shard_map/while/body/eval_jaxpr/ppermute | solution.py:85
  783.8 48.8 %collective-permute-start.3 = (bf16[2048,4,128]{2,0,1:T(8,128)(2,1)}, bf16[2048,4,128]{2,0,1:T(8,128)(2,1)}, u32[]{:S(2)}, u32[]{:S(2)}) collective-permute-start(bf16[2048,4,128]{2,0,1:T(8,128)(2,1)} %get-tuple-element.290), channel_id=1, source_target_pairs={{0,1},{1,2},{2,3},{3,4},{4,5},{5,6},{6,7},{7,0}} | collective-permute-start | bytes 6291464 | tf_op jit(solution)/shard_map/while/body/eval_jaxpr/ppermute | solution.py:86
  843.2 26.4 %collective-permute-start.2 = (bf16[2048,4,128]{2,0,1:T(8,128)(2,1)}, bf16[2048,4,128]{2,0,1:T(8,128)(2,1)S(1)}, u32[]{:S(2)}, u32[]{:S(2)}) collective-permute-start(bf16[2048,4,128]{2,0,1:T(8,128)(2,1)} %get-tuple-element.289), channel_id=1, source_target_pairs={{0,1},{1,2},{2,3},{3,4},{4,5},{5,6},{6,7},{7,0}} | collective-permute-start | bytes 6291464 | tf_op jit(solution)/shard_map/while/body/eval_jaxpr/ppermute | solution.py:85
  843.2 48.8 %collective-permute-start.3 = (bf16[2048,4,128]{2,0,1:T(8,128)(2,1)}, bf16[2048,4,128]{2,0,1:T(8,128)(2,1)}, u32[]{:S(2)}, u32[]{:S(2)}) collective-permute-start(bf16[2048,4,128]{2,0,1:T(8,128)(2,1)} %get-tuple-element.290), channel_id=1, source_target_pairs={{0,1},{1,2},{2,3},{3,4},{4,5},{5,6},{6,7},{7,0}} | collective-permute-start | bytes 6291464 | tf_op jit(solution)/shard_map/while/body/eval_jaxpr/ppermute | solution.py:86
  902.6 26.4 %collective-permute-start.2 = (bf16[2048,4,128]{2,0,1:T(8,128)(2,1)}, bf16[2048,4,128]{2,0,1:T(8,128)(2,1)S(1)}, u32[]{:S(2)}, u32[]{:S(2)}) collective-permute-start(bf16[2048,4,128]{2,0,1:T(8,128)(2,1)} %get-tuple-element.289), channel_id=1, source_target_pairs={{0,1},{1,2},{2,3},{3,4},{4,5},{5,6},{6,7},{7,0}} | collective-permute-start | bytes 6291464 | tf_op jit(solution)/shard_map/while/body/eval_jaxpr/ppermute | solution.py:85
  902.6 48.8 %collective-permute-start.3 = (bf16[2048,4,128]{2,0,1:T(8,128)(2,1)}, bf16[2048,4,128]{2,0,1:T(8,128)(2,1)}, u32[]{:S(2)}, u32[]{:S(2)}) collective-permute-start(bf16[2048,4,128]{2,0,1:T(8,128)(2,1)} %get-tuple-element.290), channel_id=1, source_target_pairs={{0,1},{1,2},{2,3},{3,4},{4,5},{5,6},{6,7},{7,0}} | collective-permute-start | bytes 6291464 | tf_op jit(solution)/shard_map/while/body/eval_jaxpr/ppermute | solution.py:86
  962.0 26.4 %collective-permute-start.2 = (bf16[2048,4,128]{2,0,1:T(8,128)(2,1)}, bf16[2048,4,128]{2,0,1:T(8,128)(2,1)S(1)}, u32[]{:S(2)}, u32[]{:S(2)}) collective-permute-start(bf16[2048,4,128]{2,0,1:T(8,128)(2,1)} %get-tuple-element.289), channel_id=1, source_target_pairs={{0,1},{1,2},{2,3},{3,4},{4,5},{5,6},{6,7},{7,0}} | collective-permute-start | bytes 6291464 | tf_op jit(solution)/shard_map/while/body/eval_jaxpr/ppermute | solution.py:85
  962.0 48.8 %collective-permute-start.3 = (bf16[2048,4,128]{2,0,1:T(8,128)(2,1)}, bf16[2048,4,128]{2,0,1:T(8,128)(2,1)}, u32[]{:S(2)}, u32[]{:S(2)}) collective-permute-start(bf16[2048,4,128]{2,0,1:T(8,128)(2,1)} %get-tuple-element.290), channel_id=1, source_target_pairs={{0,1},{1,2},{2,3},{3,4},{4,5},{5,6},{6,7},{7,0}} | collective-permute-start | bytes 6291464 | tf_op jit(solution)/shard_map/while/body/eval_jaxpr/ppermute | solution.py:86
  1021.4 26.4 %collective-permute-start.2 = (bf16[2048,4,128]{2,0,1:T(8,128)(2,1)}, bf16[2048,4,128]{2,0,1:T(8,128)(2,1)S(1)}, u32[]{:S(2)}, u32[]{:S(2)}) collective-permute-start(bf16[2048,4,128]{2,0,1:T(8,128)(2,1)} %get-tuple-element.289), channel_id=1, source_target_pairs={{0,1},{1,2},{2,3},{3,4},{4,5},{5,6},{6,7},{7,0}} | collective-permute-start | bytes 6291464 | tf_op jit(solution)/shard_map/while/body/eval_jaxpr/ppermute | solution.py:85
  1021.5 48.8 %collective-permute-start.3 = (bf16[2048,4,128]{2,0,1:T(8,128)(2,1)}, bf16[2048,4,128]{2,0,1:T(8,128)(2,1)}, u32[]{:S(2)}, u32[]{:S(2)}) collective-permute-start(bf16[2048,4,128]{2,0,1:T(8,128)(2,1)} %get-tuple-element.290), channel_id=1, source_target_pairs={{0,1},{1,2},{2,3},{3,4},{4,5},{5,6},{6,7},{7,0}} | collective-permute-start | bytes 6291464 | tf_op jit(solution)/shard_map/while/body/eval_jaxpr/ppermute | solution.py:86
  1080.9 26.4 %collective-permute-start.2 = (bf16[2048,4,128]{2,0,1:T(8,128)(2,1)}, bf16[2048,4,128]{2,0,1:T(8,128)(2,1)S(1)}, u32[]{:S(2)}, u32[]{:S(2)}) collective-permute-start(bf16[2048,4,128]{2,0,1:T(8,128)(2,1)} %get-tuple-element.289), channel_id=1, source_target_pairs={{0,1},{1,2},{2,3},{3,4},{4,5},{5,6},{6,7},{7,0}} | collective-permute-start | bytes 6291464 | tf_op jit(solution)/shard_map/while/body/eval_jaxpr/ppermute | solution.py:85
  1080.9 48.8 %collective-permute-start.3 = (bf16[2048,4,128]{2,0,1:T(8,128)(2,1)}, bf16[2048,4,128]{2,0,1:T(8,128)(2,1)}, u32[]{:S(2)}, u32[]{:S(2)}) collective-permute-start(bf16[2048,4,128]{2,0,1:T(8,128)(2,1)} %get-tuple-element.290), channel_id=1, source_target_pairs={{0,1},{1,2},{2,3},{3,4},{4,5},{5,6},{6,7},{7,0}} | collective-permute-start | bytes 6291464 | tf_op jit(solution)/shard_map/while/body/eval_jaxpr/ppermute | solution.py:86
  1141.2 12.2 %copy-start.22 = (bf16[64,4,128]{2,0,1:T(8,128)(2,1)S(1)}, bf16[64,4,128]{2,0,1:T(8,128)(2,1)}, u32[]{:S(2)}) copy-start(bf16[64,4,128]{2,0,1:T(8,128)(2,1)} %copy-done.21) | copy-start | bytes 196612
  1141.2 12.9 %copy-start.20 = (bf16[64,4,128]{2,0,1:T(8,128)(2,1)S(1)}, bf16[64,4,128]{2,0,1:T(8,128)(2,1)}, u32[]{:S(2)}) copy-start(bf16[64,4,128]{2,0,1:T(8,128)(2,1)} %copy-done.19) | copy-start | bytes 196612
  1141.2 13.6 %copy-start.18 = (bf16[64,512]{1,0:T(8,128)(2,1)S(1)}, bf16[64,512]{1,0:T(8,128)(2,1)}, u32[]{:S(2)}) copy-start(bf16[64,512]{1,0:T(8,128)(2,1)} %copy-done.17) | copy-start | bytes 196612
  (19 other events, 67.2 us)
where the time goes:
time: 1170 us; the launch traced here: 1160 us
  waiting for transfers between devices  453 us (39%)
  matrix products  433 us (37%)
  other arithmetic  131 us (11%)
  local copies, waits for them, and re-layouts  82 us (7%)
  blocking collectives  53.1 us (5%)
    ppermute x14, waiting for transfers between devices, cache_step(): blk_k = lax.ppermute(blk_k, 'cp', shift)  367 us
    reduce_sum x18, other arithmetic, partial_attend(): total = jnp.sum(prob_w, axis=-1)  126 us
    dot_general x18, matrix products, partial_attend(): jnp.einsum('tkgs,skd->tkgd', prob_w.astype(jnp.bfloat16), values, preferr...  125 us
    dot_general x18, matrix products, partial_attend(): jnp.einsum('tkgd,skd->tkgs', q_grp, keys, preferred_element_type=jnp.floa...  118 us
    ppermute x14, waiting for transfers between devices, cache_step(): blk_v = lax.ppermute(blk_v, 'cp', shift)  85.2 us
    while x56, local copies, waits for them, and re-layouts  67.9 us
    dot_general x1, matrix products, mlp_block(): jnp.dot(normed, w_up, preferred_element_type=jnp.float32)  46.9 us
    dot_general x1, matrix products, mlp_block(): jnp.dot(normed, w_gate, preferred_element_type=jnp.float32)  46.7 us
  transfers between devices with their start and end apart: 28, of which 28 were waited for; matrix products, arithmetic and copies ran while one was open for 20% of the time, Pallas kernels for 0%

commit v1 on v0

v1 whole, which is shorter than its diff:
```python
import functools

import jax
import jax.numpy as jnp
from jax import lax
from jax.experimental import pallas as pl
from jax.experimental.pallas import tpu as pltpu
from jax.sharding import PartitionSpec as P

ROPE_THETA = 500000.0
NORM_EPS = 1e-5
LOG2E = 1.4426950408889634
KV_HEADS = 4
HEAD = 128
GROUP = 7
CHIPS = 4
COL = 256
SLOTS = 2 * CHIPS
MIB = 1024 * 1024
MESH = pl.DeviceIdType.MESH


def rope_tables(positions):
    half_dim = HEAD // 2
    inv_freq = 1.0 / (ROPE_THETA ** (jnp.arange(half_dim, dtype=jnp.float32) * (2.0 / HEAD)))
    angles = positions.astype(jnp.float32)[:, None] * inv_freq[None, :]
    cos_t, sin_t = jnp.cos(angles), jnp.sin(angles)
    return jnp.concatenate([cos_t, cos_t], axis=-1), jnp.concatenate([-sin_t, sin_t], axis=-1)


def norm_rows(wide):
    return (wide * lax.rsqrt(jnp.mean(wide * wide, axis=-1, keepdims=True) + NORM_EPS)).astype(jnp.bfloat16)


def peers():
    me = lax.axis_index('cp')
    chip, core = me // 2, me % 2
    across = [2 * (chip ^ step) + core for step in range(CHIPS)]
    return chip, core, across, 2 * chip + (1 - core)


def meet(others):
    barrier = pltpu.get_barrier_semaphore()
    for dev in others:
        pl.semaphore_signal(barrier, inc=1, device_id={'cp': dev}, device_id_type=MESH)
    pl.semaphore_wait(barrier, len(others))


def remote(src, dst, send_sem, recv_sem, dev):
    return pltpu.make_async_remote_copy(src_ref=src, dst_ref=dst, send_sem=send_sem, recv_sem=recv_sem,
                                        device_id={'cp': dev}, device_id_type=MESH)


def layer_kernel(resharded, a_ref, bias_ref, cos_ref, sin_ref, k4_ref, v4_ref, *refs):
    if resharded:
        kin_ref, vin_ref, wq_ref, wk_ref, wv_ref, wo_ref = refs[:6]
        refs = refs[6:]
    else:
        wq_ref, wk_ref, wv_ref, wo_ref = refs[:4]
        refs = refs[4:]
    (y_ref, knew_ref, vnew_ref, xn, wbuf, wo, kb, vb, vt, msg, got, peer_new, newk, newvt, qt,
     s_even, s_odd, m_even, m_odd, acc, m_run, l_run, o_send, o_all,
     w_sem, wo_sem, loc_sem, kv_send, kv_recv, pair_send, pair_recv, q_send, q_recv,
     new_send, new_recv, o_ssem, o_rsem) = refs
    chip, core, across, partner = peers()
    scale2 = HEAD ** -0.5 * LOG2E
    tok = a_ref.shape[0]
    chunk = kb.shape[1]
    rows = qt.shape[2]
    n_buf = wbuf.shape[0]
    n_q, n_k = wq_ref.shape[1] // COL, wk_ref.shape[1] // COL
    n_blk = n_q + 2 * n_k
    n_items = SLOTS * GROUP

    def fetch(blk):
        slot = blk % n_buf

        @pl.when(blk < n_q)
        def _():
            pltpu.make_async_copy(wq_ref.at[:, pl.ds(blk * COL, COL)], wbuf.at[slot], w_sem.at[slot]).start()

        @pl.when((blk >= n_q) & (blk < n_q + n_k))
        def _():
            pltpu.make_async_copy(wk_ref.at[:, pl.ds((blk - n_q) * COL, COL)], wbuf.at[slot], w_sem.at[slot]).start()

        @pl.when((blk >= n_q + n_k) & (blk < n_blk))
        def _():
            pltpu.make_async_copy(wv_ref.at[:, pl.ds((blk - n_q - n_k) * COL, COL)], wbuf.at[slot], w_sem.at[slot]).start()

    for b in range(n_buf):
        pltpu.make_async_copy(wq_ref.at[:, b * COL:(b + 1) * COL], wbuf.at[b], w_sem.at[b]).start()
    meet(across[1:] + [partner])

    own = [pltpu.make_async_copy(k4_ref.at[chip], kb.at[0], loc_sem.at[0]),
           pltpu.make_async_copy(v4_ref.at[chip], vb.at[0], loc_sem.at[1])]
    for c in own:
        c.start()

    def kv_copy(step, which):
        src, dst = (k4_ref, kb) if which == 0 else (v4_ref, vb)
        return remote(src.at[chip ^ step], dst.at[2 * step], kv_send.at[step - 1, which], kv_recv.at[step - 1, which],
                      across[step])

    def pair_copy(step, which):
        dst = kb if which == 0 else vb
        if step == 0:
            src = (k4_ref if which == 0 else v4_ref).at[chip]
        else:
            src = dst.at[2 * step]
        return remote(src, dst.at[2 * step + 1], pair_send.at[step, which], pair_recv.at[step, which], partner)

    if resharded:
        loads = []
        for j in range(1, SLOTS):
            loads.append((pltpu.make_async_copy(kin_ref.at[j], kb.at[j], loc_sem.at[2 * j]),
                          pltpu.make_async_copy(vin_ref.at[j], vb.at[j], loc_sem.at[2 * j + 1])))
    else:
        for which in range(2):
            pair_copy(0, which).start()
        kv_copy(1, 0).start()
        kv_copy(2, 0).start()

    if resharded:
        xn[...] = norm_rows(a_ref[...].astype(jnp.float32))
    else:
        xn[...] = a_ref[...]

    def project(blk, carry):
        slot = blk % n_buf
        pltpu.make_async_copy(wbuf.at[slot], wbuf.at[slot], w_sem.at[slot]).wait()
        raw = (jnp.dot(xn[...], wbuf[slot], preferred_element_type=jnp.float32) + bias_ref[blk]).astype(jnp.bfloat16)
        fetch(blk + n_buf)
        is_v = blk >= n_q + n_k
        for half in range(2):
            head = 2 * blk + half
            plain = raw[:, half * HEAD:(half + 1) * HEAD]
            wide = plain.astype(jnp.float32)
            roped = (wide * cos_ref[...] + pltpu.roll(wide, HEAD // 2, 1) * sin_ref[...]).astype(jnp.bfloat16)
            value = jnp.where(is_v, plain, roped)
            is_q = blk < n_q
            kv_idx = head - 2 * n_q
            grp = jnp.where(is_q, head // GROUP, kv_idx % KV_HEADS)
            idx = jnp.where(is_q, head % GROUP, GROUP + kv_idx // KV_HEADS)
            msg[grp, idx] = value
        return carry

    lax.fori_loop(0, n_blk, project, 0)

    q_copies = [remote(msg.at[chip ^ s], got.at[s - 1], q_send.at[s - 1], q_recv.at[s - 1], across[s]) for s in range(1, CHIPS)]
    for c in q_copies:
        c.start()
    wo_load = pltpu.make_async_copy(wo_ref, wo, wo_sem)
    if resharded:
        for pair in loads:
            for c in pair:
                c.start()
    else:
        for step, which in ((1, 1), (2, 1), (3, 0), (3, 1)):
            kv_copy(step, which).start()
    wo_load.start()
    for c in range(KV_HEADS):
        knew_ref[c] = msg[c, GROUP]
        vnew_ref[c] = msg[c, GROUP + 1]
    acc[...] = jnp.zeros_like(acc)
    m_run[...] = jnp.full_like(m_run, -jnp.inf)
    l_run[...] = jnp.zeros_like(l_run)
    for c in q_copies:
        c.wait_recv()
    new_copies = [remote(msg.at[chip, pl.ds(GROUP, 2)], peer_new.at[0], new_send.at[0], new_recv.at[0], partner)]
    for s in range(1, CHIPS):
        new_copies.append(remote(got.at[s - 1, pl.ds(GROUP, 2)], peer_new.at[s], new_send.at[s], new_recv.at[s], partner))
    for c in new_copies:
        c.start()
    for g in range(GROUP):
        cols = jnp.concatenate([msg[chip, g]] + [got[s - 1, g] for s in range(1, CHIPS)], axis=0)
        qt[g] = cols.T

    def ready(j):
        for jj in range(SLOTS):
            @pl.when(j == jj)
            def _():
                if jj == 0:
                    for c in own:
                        c.wait()
                elif resharded:
                    for c in loads[jj - 1]:
                        c.wait()
                elif jj % 2 == 0:
                    for which in range(2):
                        kv_copy(jj // 2, which).wait_recv()
                        pair_copy(jj // 2, which).start()
                else:
                    for which in range(2):
                        pair_copy(jj // 2, which).wait_recv()

        vt[j % 2] = vb[j].T

    def score(item, s_dst, m_dst):
        j, g = item // GROUP, item % GROUP
        part = jnp.full((8, rows), -jnp.inf, jnp.float32)
        for t in range(chunk // 256):
            s_blk = jnp.dot(kb[j, t * 256:(t + 1) * 256, :], qt[g], preferred_element_type=jnp.float32)
            s_dst[t * 256:(t + 1) * 256, :] = s_blk
            part = jnp.maximum(part, jnp.max(s_blk.reshape(32, 8, rows), axis=0))
        m_dst[...] = part

    def absorb(item, s_src, m_src):
        j, g = item // GROUP, item % GROUP
        m_old = m_run[g]
        m_new = jnp.maximum(m_old, jnp.max(m_src[...], axis=0, keepdims=True))
        alpha = jnp.exp2((m_old - m_new) * scale2)
        shift = m_new * scale2
        l_part = jnp.zeros((8, rows), jnp.float32)
        out = jnp.zeros((HEAD, rows), jnp.float32)
        for t in range(chunk // 256):
            p = jnp.exp2(s_src[t * 256:(t + 1) * 256, :] * scale2 - shift)
            l_part = l_part + jnp.sum(p.reshape(32, 8, rows), axis=0)
            out = out + jnp.dot(vt[j % 2, :, t * 256:(t + 1) * 256], p.astype(jnp.bfloat16),
                                preferred_element_type=jnp.float32)
        acc[g] = acc[g] * alpha + out
        l_run[g] = l_run[g] * alpha + l_part
        m_run[g] = m_new

    ready(0)
    score(0, s_even, m_even)

    def pair(i, carry):
        first = 2 * i
        nxt = first + 2

        @pl.when((first + 1) % GROUP == 0)
        def _():
            ready((first + 1) // GROUP)

        @pl.when((nxt % GROUP == 0) & (nxt < n_items))
        def _():
            ready(nxt // GROUP)

        score(first + 1, s_odd, m_odd)
        absorb(first, s_even, m_even)
        score(jnp.minimum(nxt, n_items - 1), s_even, m_even)
        absorb(first + 1, s_odd, m_odd)
        return carry

    lax.fori_loop(0, n_items // 2, pair, 0)

    for c in new_copies:
        c.wait_recv()
    for s in range(CHIPS):
        mine = (msg.at[chip], GROUP) if s == 0 else (got.at[s - 1], GROUP)
        for r in range(2):
            at = (r * CHIPS + s) * tok
            if r == 0:
                nk, nv = mine[0][mine[1]], mine[0][mine[1] + 1]
            else:
                nk, nv = peer_new[s, 0], peer_new[s, 1]
            newk[at:at + tok, :] = nk
            newvt[at:at + tok, :] = nv

    new_len = newk.shape[0]
    key_i = lax.broadcasted_iota(jnp.int32, (new_len, rows), 0)
    qry_i = lax.broadcasted_iota(jnp.int32, (new_len, rows), 1)
    blk = key_i // tok
    k_pos = (2 * (chip ^ (blk % CHIPS)) + (core ^ (blk // CHIPS))) * tok + key_i % tok
    q_pos = (2 * (chip ^ (qry_i // tok)) + core) * tok + qry_i % tok
    visible = k_pos <= q_pos

    for g in range(GROUP):
        s = jnp.dot(newk[...], qt[g], preferred_element_type=jnp.float32)
        s = jnp.where(visible, s, -jnp.inf)
        m_old = m_run[g]
        m_new = jnp.maximum(m_old, jnp.max(s, axis=0, keepdims=True))
        alpha = jnp.exp2((m_old - m_new) * scale2)
        p = jnp.exp2(s * scale2 - m_new * scale2)
        total = jnp.sum(l_run[g] * alpha, axis=0, keepdims=True) + jnp.sum(p, axis=0, keepdims=True)
        fresh = lax.dot_general(newvt[...], p.astype(jnp.bfloat16), (((0,), (0,)), ((), ())),
                                preferred_element_type=jnp.float32)
        out = ((acc[g] * alpha + fresh) / total).T.astype(jnp.bfloat16)
        for s_i in range(CHIPS):
            o_send[s_i, :, g * HEAD:(g + 1) * HEAD] = out[s_i * tok:(s_i + 1) * tok, :]

    wide_cols = GROUP * HEAD
    here = pl.ds(pl.multiple_of(chip * wide_cols, HEAD), wide_cols)
    o_copies = [remote(o_send.at[s], o_all.at[:, here], o_ssem.at[s - 1], o_rsem.at[s - 1], across[s]) for s in range(1, CHIPS)]
    for c in o_copies:
        c.start()
    o_all[:, here] = o_send[0]
    wo_load.wait()
    for c in o_copies:
        c.wait_recv()

    def out_proj(blk, carry):
        cols = pl.ds(pl.multiple_of(blk * COL, COL), COL)
        y = jnp.dot(o_all[...], wo[:, cols], preferred_element_type=jnp.float32).astype(jnp.bfloat16)
        if not resharded:
            y = (a_ref[:, cols].astype(jnp.float32) + y.astype(jnp.float32)).astype(jnp.bfloat16)
        y_ref[:, cols] = y
        return carry

    lax.fori_loop(0, wo.shape[1] // COL, out_proj, 0)

    for c in q_copies + new_copies + o_copies:
        c.wait_send()
    if not resharded:
        for step in range(CHIPS):
            for which in range(2):
                pair_copy(step, which).wait_send()
                if step:
                    kv_copy(step, which).wait_send()


def run_layer(a, bias, cos_t, sin_t, k4, v4, k_in, v_in, w_q, w_k, w_v, w_o, collective_id):
    resharded = k_in is not None
    tok, width = a.shape
    chunk = k4.shape[1]
    rows = CHIPS * tok
    bf16, f32 = jnp.bfloat16, jnp.float32
    vmem = pl.BlockSpec(memory_space=pltpu.VMEM)
    hbm = pl.BlockSpec(memory_space=pl.ANY)
    dma = pltpu.SemaphoreType.DMA
    caches = (k4, v4, k_in, v_in) if resharded else (k4, v4)
    return pl.pallas_call(
        functools.partial(layer_kernel, resharded),
        out_shape=[jax.ShapeDtypeStruct((tok, width), bf16),
                   jax.ShapeDtypeStruct((KV_HEADS, tok, HEAD), bf16),
                   jax.ShapeDtypeStruct((KV_HEADS, tok, HEAD), bf16)],
        in_specs=[vmem] * 4 + [hbm] * (len(caches) + 4),
        out_specs=[vmem] * 3,
        scratch_shapes=[
            pltpu.VMEM((tok, width), bf16),
            pltpu.VMEM((4, width, COL), bf16),
            pltpu.VMEM(w_o.shape, bf16),
            pltpu.VMEM((SLOTS, chunk, HEAD), bf16),
            pltpu.VMEM((SLOTS, chunk, HEAD), bf16),
            pltpu.VMEM((2, HEAD, chunk), bf16),
            pltpu.VMEM((KV_HEADS, GROUP + 2, tok, HEAD), bf16),
            pltpu.VMEM((CHIPS - 1, GROUP + 2, tok, HEAD), bf16),
            pltpu.VMEM((CHIPS, 2, tok, HEAD), bf16),
            pltpu.VMEM((2 * rows, HEAD), bf16),
            pltpu.VMEM((2 * rows, HEAD), bf16),
            pltpu.VMEM((GROUP, HEAD, rows), bf16),
            pltpu.VMEM((chunk, rows), f32),
            pltpu.VMEM((chunk, rows), f32),
            pltpu.VMEM((8, rows), f32),
            pltpu.VMEM((8, rows), f32),
            pltpu.VMEM((GROUP, HEAD, rows), f32),
            pltpu.VMEM((GROUP, 1, rows), f32),
            pltpu.VMEM((GROUP, 8, rows), f32),
            pltpu.VMEM((CHIPS, tok, GROUP * HEAD), bf16),
            pltpu.VMEM((tok, CHIPS * GROUP * HEAD), bf16),
            dma((4,)), dma, dma((2 * SLOTS,)),
            dma((CHIPS - 1, 2)), dma((CHIPS - 1, 2)), dma((CHIPS, 2)), dma((CHIPS, 2)),
            dma((CHIPS - 1,)), dma((CHIPS - 1,)), dma((CHIPS,)), dma((CHIPS,)),
            dma((CHIPS - 1,)), dma((CHIPS - 1,)),
        ],
        compiler_params=pltpu.CompilerParams(collective_id=collective_id, has_side_effects=True, vmem_limit_bytes=60 * MIB),
        name="layer",
    )(a, bias, cos_t, sin_t, *caches, w_q, w_k, w_v, w_o)


def mlp_kernel(h_ref, k4_ref, v4_ref, gate_ref, up_ref, down_ref, g_ref, kout_ref, vout_ref,
               u, wg, wu, wd, acc, theirs, w_sem, u_send, u_recv, part_send, part_recv, kv_send, kv_recv, pair_send, pair_recv):
    chip, core, across, partner = peers()
    tok = h_ref.shape[0]
    n_buf = wg.shape[0]
    steps = gate_ref.shape[1] // (2 * COL)

    def copies(i):
        slot = i % n_buf
        cols = pl.ds(pl.multiple_of((core * steps + i) * COL, COL), COL)
        return (pltpu.make_async_copy(gate_ref.at[:, cols], wg.at[slot], w_sem.at[slot, 0]),
                pltpu.make_async_copy(up_ref.at[:, cols], wu.at[slot], w_sem.at[slot, 1]),
                pltpu.make_async_copy(down_ref.at[cols, :], wd.at[slot], w_sem.at[slot, 2]))

    for b in range(n_buf):
        for c in copies(b):
            c.start()
    meet(across[1:] + [partner])
    u[:tok, :] = norm_rows(h_ref[...].astype(jnp.float32))
    u_copy = remote(u.at[pl.ds(0, tok)], u.at[pl.ds(tok, tok)], u_send, u_recv, partner)
    u_copy.start()

    def kv_copy(step, which):
        src, dst = (k4_ref, kout_ref) if which == 0 else (v4_ref, vout_ref)
        return remote(src.at[chip ^ step], dst.at[2 * step], kv_send.at[step - 1, which], kv_recv.at[step - 1, which],
                      across[step])

    def pair_copy(step, which):
        dst = kout_ref if which == 0 else vout_ref
        src = (k4_ref if which == 0 else v4_ref).at[chip] if step == 0 else dst.at[2 * step]
        return remote(src, dst.at[2 * step + 1], pair_send.at[step, which], pair_recv.at[step, which], partner)

    for step in range(1, CHIPS):
        for which in range(2):
            kv_copy(step, which).start()
    for which in range(2):
        pair_copy(0, which).start()
    acc[...] = jnp.zeros_like(acc)
    u_copy.wait_recv()

    def relay(step):
        for which in range(2):
            kv_copy(step, which).wait_recv()
            pair_copy(step, which).start()

    def block(i, carry):
        slot = i % n_buf
        for c in copies(i):
            c.wait()
        gate = jnp.dot(u[...], wg[slot], preferred_element_type=jnp.float32).astype(jnp.bfloat16).astype(jnp.float32)
        up = jnp.dot(u[...], wu[slot], preferred_element_type=jnp.float32).astype(jnp.bfloat16).astype(jnp.float32)
        mixed = (gate * jax.nn.sigmoid(gate) * up).astype(jnp.bfloat16)
        acc[...] += jnp.dot(mixed, wd[slot], preferred_element_type=jnp.float32)

        @pl.when(i + n_buf < steps)
        def _():
            for c in copies(i + n_buf):
                c.start()

        @pl.when(i == steps - 12)
        def _():
            relay(1)
            relay(2)

        @pl.when(i == steps - 5)
        def _():
            relay(3)

        return carry

    lax.fori_loop(0, steps, block, 0)
    part_copy = remote(acc.at[pl.ds(tok, tok)], theirs, part_send, part_recv, partner)
    part_copy.start()
    part_copy.wait_recv()
    g_ref[...] = (h_ref[...].astype(jnp.float32) + (acc[:tok, :] + theirs[...])).astype(jnp.bfloat16)
    for step in range(CHIPS):
        for which in range(2):
            pair_copy(step, which).wait()
            if step:
                kv_copy(step, which).wait_send()
    u_copy.wait_send()
    part_copy.wait_send()


def run_mlp(h, k4, v4, w_gate, w_up, w_down, collective_id):
    tok, width = h.shape
    chunk = k4.shape[1]
    bf16, f32 = jnp.bfloat16, jnp.float32
    vmem = pl.BlockSpec(memory_space=pltpu.VMEM)
    hbm = pl.BlockSpec(memory_space=pl.ANY)
    dma = pltpu.SemaphoreType.DMA
    n_buf = 4
    slots = jax.ShapeDtypeStruct((SLOTS, chunk, HEAD), bf16)
    return pl.pallas_call(
        mlp_kernel,
        out_shape=[jax.ShapeDtypeStruct((tok, width), bf16), slots, slots],
        in_specs=[vmem] + [hbm] * 5,
        out_specs=[vmem, hbm, hbm],
        scratch_shapes=[
            pltpu.VMEM((2 * tok, width), bf16),
            pltpu.VMEM((n_buf, width, COL), bf16),
            pltpu.VMEM((n_buf, width, COL), bf16),
            pltpu.VMEM((n_buf, COL, width), bf16),
            pltpu.VMEM((2 * tok, width), f32),
            pltpu.VMEM((tok, width), f32),
            dma((n_buf, 3)), dma, dma, dma, dma,
            dma((CHIPS - 1, 2)), dma((CHIPS - 1, 2)), dma((CHIPS, 2)), dma((CHIPS, 2)),
        ],
        compiler_params=pltpu.CompilerParams(collective_id=collective_id, has_side_effects=True, vmem_limit_bytes=60 * MIB),
        name="mlp",
    )(h, k4, v4, w_gate, w_up, w_down)


def heads_first(cache):
    return lax.optimization_barrier(jnp.transpose(cache, (1, 0, 2)))


def pack_bias(b_q, b_k):
    wide = jnp.concatenate([b_q.astype(jnp.float32), b_k.astype(jnp.float32), jnp.zeros(b_k.shape, jnp.float32)])
    return wide.reshape(-1, 1, COL)


def solution(mesh):
    axis_size = mesh.shape['cp']
    rows_spec = P(('dp', 'cp'), None)
    cache_spec = P(('dp', 'cp'), None, None)
    mat_spec = P(None, None)
    vec_spec = P(None)
    layer_specs = (cache_spec, cache_spec, mat_spec, vec_spec, mat_spec, vec_spec, mat_spec, mat_spec)
    in_specs = (rows_spec,) + layer_specs + (mat_spec, mat_spec, mat_spec) + layer_specs
    out_specs = (rows_spec, rows_spec, cache_spec, cache_spec, cache_spec, cache_spec)

    def forward(x_in, cache_k1, cache_v1, w_q1, b_q1, w_k1, b_k1, w_v1, w_o1, w_gate, w_up, w_down, cache_k2, cache_v2, w_q2, b_q2, w_k2, b_k2, w_v2, w_o2):
        me = lax.axis_index('cp')
        tok = x_in.shape[0]
        positions = axis_size * cache_k1.shape[0] + me * tok + jnp.arange(tok)
        cos_t, sin_t = rope_tables(positions)
        k4a, v4a = heads_first(cache_k1), heads_first(cache_v1)
        k4b, v4b = heads_first(cache_k2), heads_first(cache_v2)
        resid_h, k_one, v_one = run_layer(x_in, pack_bias(b_q1, b_k1), cos_t, sin_t, k4a, v4a, None, None,
                                          w_q1, w_k1, w_v1, w_o1, 1)
        hidden, k_in, v_in = run_mlp(resid_h, k4b, v4b, w_gate, w_up, w_down, 2)
        y_two, k_two, v_two = run_layer(hidden, pack_bias(b_q2, b_k2), cos_t, sin_t, k4b, v4b, k_in, v_in,
                                        w_q2, w_k2, w_v2, w_o2, 3)
        back = lambda t: jnp.transpose(t, (1, 0, 2))
        return hidden, y_two, back(k_one), back(v_one), back(k_two), back(v_two)

    return jax.shard_map(forward, mesh=mesh, in_specs=in_specs, out_specs=out_specs, check_vma=False)
```

time: 1170 us -> 262 us (0.22); the launches traced: 1160 us -> 262 us
  waiting for transfers between devices: 453 us -> 0 us
  matrix products: 433 us -> 0 us
  Pallas kernels: 0 us -> 239 us
  other arithmetic: 131 us -> 3.84 us
  local copies, waits for them, and re-layouts: 82 us -> 18.1 us
  blocking collectives: 53.1 us -> 0 us
    ppermute x28 -> x0, waiting for transfers between devices: 453 us -> none  [the longest x14 367 us: cache_step(): blk_k = lax.ppermute(blk_k, 'cp', shift)]
    dot_general x47 -> x0, matrix products: 433 us -> none  [the longest x18 125 us: partial_attend(): jnp.einsum('tkgs,skd->tkgd', prob_w.astype(jnp.bfloat16), values, preferr...]
    pallas_call x0 -> x3, Pallas kernels: none -> 239 us  [the longest x2 172 us: run_layer(): pl.pallas_call(functools.partial(layer_kernel, resharded), out_shape=[jax...]
    reduce_sum x18 -> x0, other arithmetic: 126 us -> none  [partial_attend(): total = jnp.sum(prob_w, axis=-1)]
    while x60 -> x0, local copies, waits for them, and re-layouts: 74.3 us -> none
    all_gather x4 -> x0, blocking collectives: 53.1 us -> none  [the longest x2 28 us: attention_layer(): all_k = lax.all_gather(k_new, 'cp', axis=0, tiled=True)]
    unnamed x52 -> x18, local copies, waits for them, and re-layouts: 3.32 us -> 16.9 us
  transfers between devices with their start and end apart: 28 -> 0, of which waited for: 28 -> 0; matrix products, arithmetic and copies ran while one was open for 20% -> 0% of each run, Pallas kernels for 0% -> 0%
where the time goes in v1:
time: 262 us
  Pallas kernels  239 us (91%)
  local copies, waits for them, and re-layouts  18.1 us (7%)
  other arithmetic  3.84 us (1%)
    pallas_call x2, Pallas kernels, run_layer(): pl.pallas_call(functools.partial(layer_kernel, resharded), out_shape=[jax...  172 us
    pallas_call x1, Pallas kernels, run_mlp(): pl.pallas_call(mlp_kernel, out_shape=[jax.ShapeDtypeStruct((tok, width),...  66.5 us
    unnamed x18, local copies, waits for them, and re-layouts  16.9 us

profile of v1, /device:TPU:0, one launch (start us, length us, event | category | flops | bytes accessed | tf_op | source)
XLA Modules:
  0.0 261.6 jit_solution(11491148929490314978)
XLA Ops:
  0.6 0.0 copy-start
  0.7 0.8 convert_element_type.20
  1.5 0.7 convert_element_type.23
  2.2 0.7 convert_element_type.19
  2.9 0.7 convert_element_type.22
  3.6 0.6 reshape.30.bias_ref
  4.2 0.6 reshape.29.bias_ref
  4.8 0.2 fusion
  5.0 0.7 pad_maximum_fusion
  5.8 3.2 %copy.41 = bf16[2048,4,128]{2,0,1:T(8,128)(2,1)} copy(bf16[2048,4,128]{2,1,0:T(4,128)(2,1)} %param.21) | data formatting | bytes 4194304 | tf_op args[1]
  9.0 0.0 copy-done
  9.0 1.6 copy.40
  10.5 0.0 copy-start.1
  10.6 88.1 %layer.2 = (bf16[64,3584]{1,0:T(8,128)(2,1)}, bf16[4,64,128]{2,1,0:T(8,128)(2,1)}, bf16[4,64,128]{2,1,0:T(8,128)(2,1)}) custom-call(bf16[64,3584]{1,0:T(8,128)(2,1)} %a_ref.1, f32[18,1,256]{2,1,0:T(1,128)} %reshape.29.bias_ref, f32[64,128]{1,0:T(8,128)} %get-tuple-element.35.cos_ref, f32[64,128]{1,0:T(8,128)} %get-tuple-element.36.sin_ref, ...), custom_call_target="tpu_custom_call" | custom-call | tf_op jit(solution)/shard_map/layer/pallas_call | solution.py:322
  98.7 0.0 copy-start.2
  98.7 1.7 copy.30
  100.4 1.5 copy.31
  101.9 0.0 copy-done.1
  101.9 1.6 copy.39
  103.5 0.0 copy-done.2
  103.5 1.6 copy.38
  105.1 66.5 %mlp.1 = (bf16[64,3584]{1,0:T(8,128)(2,1)}, bf16[8,2048,128]{2,1,0:T(8,128)(2,1)}, bf16[8,2048,128]{2,1,0:T(8,128)(2,1)}) custom-call(bf16[64,3584]{1,0:T(8,128)(2,1)} %get-tuple-element.15.h_ref, bf16[4,2048,128]{2,1,0:T(8,128)(2,1)} %bitcast.16, bf16[4,2048,128]{2,1,0:T(8,128)(2,1)} %bitcast.18, bf16[3584,18944]{1,0:T(8,128)(2,1)} %gate_ref.1, ...), custom_call_target="tpu_custom_call" | custom-call | tf_op jit(solution)/shard_map/mlp/pallas_call | solution.py:454
  171.6 0.0 copy-start.3
  171.7 84.3 %layer.3 = (bf16[64,3584]{1,0:T(8,128)(2,1)}, bf16[4,64,128]{2,1,0:T(8,128)(2,1)}, bf16[4,64,128]{2,1,0:T(8,128)(2,1)}) custom-call(bf16[64,3584]{1,0:T(8,128)(2,1)} %get-tuple-element.43.a_ref, f32[18,1,256]{2,1,0:T(1,128)} %reshape.30.bias_ref, f32[64,128]{1,0:T(8,128)} %get-tuple-element.35.cos_ref, f32[64,128]{1,0:T(8,128)} %get-tuple-element.36.sin_ref, ...), custom_call_target="tpu_custom_call" | custom-call | tf_op jit(solution)/shard_map/layer/pallas_call | solution.py:322
  256.0 1.5 copy.32
  257.5 1.5 copy.33
  259.0 0.0 copy-done.3
  259.0 0.8 copy.44
  259.8 1.8 copy.45
  (4 shorter events, 0.0 us)
Async XLA Ops:
  0.6 8.3 %copy-start = (bf16[2048,4,128]{2,1,0:T(4,128)(2,1)S(1)}, bf16[2048,4,128]{2,1,0:T(4,128)(2,1)}, u32[]{:S(2)}) copy-start(bf16[2048,4,128]{2,1,0:T(4,128)(2,1)} %param.22) | copy-start | bytes 6291460
  10.5 91.4 %copy-start.1 = (bf16[2048,4,128]{2,1,0:T(4,128)(2,1)S(1)}, bf16[2048,4,128]{2,1,0:T(4,128)(2,1)}, u32[]{:S(2)}) copy-start(bf16[2048,4,128]{2,1,0:T(4,128)(2,1)} %param.32) | copy-start | bytes 6291460
  98.7 4.8 %copy-start.2 = (bf16[2048,4,128]{2,1,0:T(4,128)(2,1)S(1)}, bf16[2048,4,128]{2,1,0:T(4,128)(2,1)}, u32[]{:S(2)}) copy-start(bf16[2048,4,128]{2,1,0:T(4,128)(2,1)} %param.33) | copy-start | bytes 6291460
  171.6 87.4 %copy-start.3 = (bf16[64,3584]{1,0:T(8,128)(2,1)S(1)}, bf16[64,3584]{1,0:T(8,128)(2,1)}, u32[]{:S(2)}) copy-start(bf16[64,3584]{1,0:T(8,128)(2,1)} %get-tuple-element.43.a_ref) | copy-start | bytes 1376260

commit v2 on v1

--- a/solution.py
+++ b/solution.py
@@ -2,6 +2,7 @@
 
 import jax
 import jax.numpy as jnp
+import numpy as np
 from jax import lax
 from jax.experimental import pallas as pl
 from jax.experimental.pallas import tpu as pltpu
@@ -20,12 +21,14 @@
 MESH = pl.DeviceIdType.MESH
 
 
-def rope_tables(positions):
-    half_dim = HEAD // 2
-    inv_freq = 1.0 / (ROPE_THETA ** (jnp.arange(half_dim, dtype=jnp.float32) * (2.0 / HEAD)))
-    angles = positions.astype(jnp.float32)[:, None] * inv_freq[None, :]
-    cos_t, sin_t = jnp.cos(angles), jnp.sin(angles)
-    return jnp.concatenate([cos_t, cos_t], axis=-1), jnp.concatenate([-sin_t, sin_t], axis=-1)
+@functools.lru_cache(maxsize=None)
+def rope_table(first, count):
+    with jax.ensure_compile_time_eval():
+        half_dim = HEAD // 2
+        inv_freq = 1.0 / (ROPE_THETA ** (jnp.arange(half_dim, dtype=jnp.float32) * (2.0 / HEAD)))
+        angles = (first + jnp.arange(count)).astype(jnp.float32)[:, None] * inv_freq[None, :]
+        cos_t, sin_t = jnp.cos(angles), jnp.sin(angles)
+        return np.asarray(jnp.concatenate([cos_t, cos_t, -sin_t, sin_t], axis=-1))
 
 
 def norm_rows(wide):
@@ -51,44 +54,38 @@
                                         device_id={'cp': dev}, device_id_type=MESH)
 
 
-def layer_kernel(resharded, a_ref, bias_ref, cos_ref, sin_ref, k4_ref, v4_ref, *refs):
+def layer_kernel(resharded, a_ref, bias_ref, trig_ref, k4_ref, v4_ref, *refs):
     if resharded:
         kin_ref, vin_ref, wq_ref, wk_ref, wv_ref, wo_ref = refs[:6]
         refs = refs[6:]
     else:
         wq_ref, wk_ref, wv_ref, wo_ref = refs[:4]
         refs = refs[4:]
-    (y_ref, knew_ref, vnew_ref, xn, wbuf, wo, kb, vb, vt, msg, got, peer_new, newk, newvt, qt,
+    (y_ref, knew_ref, vnew_ref, xn, trig, wkv, wo, kb, vb, vt, msg, got, peer_new, newk, newv, qt,
      s_even, s_odd, m_even, m_odd, acc, m_run, l_run, o_send, o_all,
-     w_sem, wo_sem, loc_sem, kv_send, kv_recv, pair_send, pair_recv, q_send, q_recv,
+     trig_sem, w_sem, wo_sem, loc_sem, kv_send, kv_recv, pair_send, pair_recv, q_send, q_recv,
      new_send, new_recv, o_ssem, o_rsem) = refs
     chip, core, across, partner = peers()
+    me = 2 * chip + core
     scale2 = HEAD ** -0.5 * LOG2E
     tok = a_ref.shape[0]
     chunk = kb.shape[1]
     rows = qt.shape[2]
-    n_buf = wbuf.shape[0]
-    n_q, n_k = wq_ref.shape[1] // COL, wk_ref.shape[1] // COL
-    n_blk = n_q + 2 * n_k
+    wide_cols = GROUP * HEAD
+    n_q = wq_ref.shape[1]
     n_items = SLOTS * GROUP
-
-    def fetch(blk):
-        slot = blk % n_buf
-
-        @pl.when(blk < n_q)
-        def _():
-            pltpu.make_async_copy(wq_ref.at[:, pl.ds(blk * COL, COL)], wbuf.at[slot], w_sem.at[slot]).start()
-
-        @pl.when((blk >= n_q) & (blk < n_q + n_k))
-        def _():
-            pltpu.make_async_copy(wk_ref.at[:, pl.ds((blk - n_q) * COL, COL)], wbuf.at[slot], w_sem.at[slot]).start()
-
-        @pl.when((blk >= n_q + n_k) & (blk < n_blk))
-        def _():
-            pltpu.make_async_copy(wv_ref.at[:, pl.ds((blk - n_q - n_k) * COL, COL)], wbuf.at[slot], w_sem.at[slot]).start()
-
-    for b in range(n_buf):
-        pltpu.make_async_copy(wq_ref.at[:, b * COL:(b + 1) * COL], wbuf.at[b], w_sem.at[b]).start()
+    n_first = (SLOTS - 2) * GROUP
+    bias_at = (n_q + wk_ref.shape[1]) if resharded else 0
+
+    def wq_copy(n):
+        cols = pl.ds(pl.multiple_of((chip ^ (CHIPS - 1 - n)) * wide_cols, HEAD), wide_cols)
+        return pltpu.make_async_copy(wq_ref.at[:, cols], wo.at[:, n * wide_cols:(n + 1) * wide_cols], w_sem.at[2 + n])
+
+    kv_loads = [pltpu.make_async_copy(wk_ref, wkv.at[0], w_sem.at[0]), pltpu.make_async_copy(wv_ref, wkv.at[1], w_sem.at[1])]
+    trig_load = pltpu.make_async_copy(trig_ref.at[pl.ds(me * tok, tok)], trig, trig_sem)
+    trig_load.start()
+    for c in kv_loads + [wq_copy(n) for n in range(CHIPS)]:
+        c.start()
     meet(across[1:] + [partner])
 
     own = [pltpu.make_async_copy(k4_ref.at[chip], kb.at[0], loc_sem.at[0]),
@@ -125,30 +122,45 @@
     else:
         xn[...] = a_ref[...]
 
-    def project(blk, carry):
-        slot = blk % n_buf
-        pltpu.make_async_copy(wbuf.at[slot], wbuf.at[slot], w_sem.at[slot]).wait()
-        raw = (jnp.dot(xn[...], wbuf[slot], preferred_element_type=jnp.float32) + bias_ref[blk]).astype(jnp.bfloat16)
-        fetch(blk + n_buf)
-        is_v = blk >= n_q + n_k
-        for half in range(2):
-            head = 2 * blk + half
-            plain = raw[:, half * HEAD:(half + 1) * HEAD]
-            wide = plain.astype(jnp.float32)
-            roped = (wide * cos_ref[...] + pltpu.roll(wide, HEAD // 2, 1) * sin_ref[...]).astype(jnp.bfloat16)
-            value = jnp.where(is_v, plain, roped)
-            is_q = blk < n_q
-            kv_idx = head - 2 * n_q
-            grp = jnp.where(is_q, head // GROUP, kv_idx % KV_HEADS)
-            idx = jnp.where(is_q, head % GROUP, GROUP + kv_idx // KV_HEADS)
-            msg[grp, idx] = value
+    trig_load.wait()
+
+    def rope(plain):
+        wide = plain.astype(jnp.float32)
+        return (wide * trig[:, :HEAD] + pltpu.roll(wide, HEAD // 2, 1) * trig[:, HEAD:]).astype(jnp.bfloat16)
+
+    kv_loads[0].wait()
+    k_pre = (jnp.dot(xn[...], wkv[0], preferred_element_type=jnp.float32)
+             + bias_ref[:, bias_at + n_q:bias_at + n_q + KV_HEADS * HEAD]).astype(jnp.bfloat16)
+    for c in range(KV_HEADS):
+        knew_ref[c] = rope(k_pre[:, c * HEAD:(c + 1) * HEAD])
+    kv_loads[1].wait()
+    v_pre = jnp.dot(xn[...], wkv[1], preferred_element_type=jnp.float32).astype(jnp.bfloat16)
+    for c in range(KV_HEADS):
+        vnew_ref[c] = v_pre[:, c * HEAD:(c + 1) * HEAD]
+
+    def q_copy(n):
+        return remote(msg.at[n], got.at[n], q_send.at[n], q_recv.at[n], 2 * (chip ^ (CHIPS - 1 - n)) + core)
+
+    def project(n, carry):
+        pltpu.make_async_copy(wo.at[:, :wide_cols], wo.at[:, :wide_cols], w_sem.at[2 + n]).wait()
+        grp = chip ^ (CHIPS - 1 - n)
+        cols = pl.ds(pl.multiple_of(n * wide_cols, HEAD), wide_cols)
+        bias = bias_ref[:, pl.ds(pl.multiple_of(bias_at + grp * wide_cols, HEAD), wide_cols)]
+        q_pre = (jnp.dot(xn[...], wo[:, cols], preferred_element_type=jnp.float32) + bias).astype(jnp.bfloat16)
+        for g in range(GROUP):
+            msg[n, g] = rope(q_pre[:, g * HEAD:(g + 1) * HEAD])
+        msg[n, GROUP] = knew_ref[grp]
+        msg[n, GROUP + 1] = vnew_ref[grp]
+
+        @pl.when(n < CHIPS - 1)
+        def _():
+            q_copy(n).start()
+
         return carry
 
-    lax.fori_loop(0, n_blk, project, 0)
-
-    q_copies = [remote(msg.at[chip ^ s], got.at[s - 1], q_send.at[s - 1], q_recv.at[s - 1], across[s]) for s in range(1, CHIPS)]
-    for c in q_copies:
-        c.start()
+    lax.fori_loop(0, CHIPS, project, 0)
+    q_copies = [q_copy(n) for n in range(CHIPS - 1)]
+    parts = [msg.at[CHIPS - 1]] + [got.at[CHIPS - 1 - s] for s in range(1, CHIPS)]
     wo_load = pltpu.make_async_copy(wo_ref, wo, wo_sem)
     if resharded:
         for pair in loads:
@@ -158,22 +170,19 @@
         for step, which in ((1, 1), (2, 1), (3, 0), (3, 1)):
             kv_copy(step, which).start()
     wo_load.start()
-    for c in range(KV_HEADS):
-        knew_ref[c] = msg[c, GROUP]
-        vnew_ref[c] = msg[c, GROUP + 1]
     acc[...] = jnp.zeros_like(acc)
     m_run[...] = jnp.full_like(m_run, -jnp.inf)
     l_run[...] = jnp.zeros_like(l_run)
     for c in q_copies:
         c.wait_recv()
-    new_copies = [remote(msg.at[chip, pl.ds(GROUP, 2)], peer_new.at[0], new_send.at[0], new_recv.at[0], partner)]
-    for s in range(1, CHIPS):
-        new_copies.append(remote(got.at[s - 1, pl.ds(GROUP, 2)], peer_new.at[s], new_send.at[s], new_recv.at[s], partner))
+    new_copies = [remote(parts[s].at[pl.ds(GROUP, 2)], peer_new.at[s], new_send.at[s], new_recv.at[s], partner) for s in range(CHIPS)]
     for c in new_copies:
         c.start()
     for g in range(GROUP):
-        cols = jnp.concatenate([msg[chip, g]] + [got[s - 1, g] for s in range(1, CHIPS)], axis=0)
-        qt[g] = cols.T
+        qt[g] = jnp.concatenate([p[g] for p in parts], axis=0).T
+    for s in range(CHIPS):
+        newk[s * tok:(s + 1) * tok, :] = parts[s][GROUP]
+        newv[s * tok:(s + 1) * tok, :] = parts[s][GROUP + 1]
 
     def ready(j):
         for jj in range(SLOTS):
@@ -195,8 +204,13 @@
 
         vt[j % 2] = vb[j].T
 
+    def place(item):
+        late = item - n_first
+        is_late = late >= 0
+        return jnp.where(is_late, SLOTS - 2 + late % 2, item // GROUP), jnp.where(is_late, late // 2, item % GROUP)
+
     def score(item, s_dst, m_dst):
-        j, g = item // GROUP, item % GROUP
+        j, g = place(item)
         part = jnp.full((8, rows), -jnp.inf, jnp.float32)
         for t in range(chunk // 256):
             s_blk = jnp.dot(kb[j, t * 256:(t + 1) * 256, :], qt[g], preferred_element_type=jnp.float32)
@@ -205,7 +219,7 @@
         m_dst[...] = part
 
     def absorb(item, s_src, m_src):
-        j, g = item // GROUP, item % GROUP
+        j, g = place(item)
         m_old = m_run[g]
         m_new = jnp.maximum(m_old, jnp.max(m_src[...], axis=0, keepdims=True))
         alpha = jnp.exp2((m_old - m_new) * scale2)
@@ -224,67 +238,74 @@
     ready(0)
     score(0, s_even, m_even)
 
-    def pair(i, carry):
-        first = 2 * i
-        nxt = first + 2
-
-        @pl.when((first + 1) % GROUP == 0)
-        def _():
-            ready((first + 1) // GROUP)
-
-        @pl.when((nxt % GROUP == 0) & (nxt < n_items))
-        def _():
-            ready(nxt // GROUP)
-
-        score(first + 1, s_odd, m_odd)
-        absorb(first, s_even, m_even)
-        score(jnp.minimum(nxt, n_items - 1), s_even, m_even)
-        absorb(first + 1, s_odd, m_odd)
-        return carry
-
-    lax.fori_loop(0, n_items // 2, pair, 0)
-
-    for c in new_copies:
-        c.wait_recv()
-    for s in range(CHIPS):
-        mine = (msg.at[chip], GROUP) if s == 0 else (got.at[s - 1], GROUP)
-        for r in range(2):
-            at = (r * CHIPS + s) * tok
-            if r == 0:
-                nk, nv = mine[0][mine[1]], mine[0][mine[1] + 1]
-            else:
-                nk, nv = peer_new[s, 0], peer_new[s, 1]
-            newk[at:at + tok, :] = nk
-            newvt[at:at + tok, :] = nv
-
     new_len = newk.shape[0]
-    key_i = lax.broadcasted_iota(jnp.int32, (new_len, rows), 0)
-    qry_i = lax.broadcasted_iota(jnp.int32, (new_len, rows), 1)
-    blk = key_i // tok
-    k_pos = (2 * (chip ^ (blk % CHIPS)) + (core ^ (blk // CHIPS))) * tok + key_i % tok
-    q_pos = (2 * (chip ^ (qry_i // tok)) + core) * tok + qry_i % tok
-    visible = k_pos <= q_pos
-
-    for g in range(GROUP):
+
+    def visible():
+        key_i = lax.broadcasted_iota(jnp.int32, (new_len, rows), 0)
+        qry_i = lax.broadcasted_iota(jnp.int32, (new_len, rows), 1)
+        blk = key_i // tok
+        k_pos = (2 * (chip ^ (blk % CHIPS)) + (core ^ (blk // CHIPS))) * tok + key_i % tok
+        q_pos = (2 * (chip ^ (qry_i // tok)) + core) * tok + qry_i % tok
+        return k_pos <= q_pos
+
+    def o_copy(g, s):
+        src = o_send.at[g, s]
+        dst = o_all.at[:, pl.ds(pl.multiple_of(chip * wide_cols + g * HEAD, HEAD), HEAD)]
+        return remote(src, dst, o_ssem.at[g, s - 1], o_rsem.at[g, s - 1], across[s])
+
+    def finish(g):
         s = jnp.dot(newk[...], qt[g], preferred_element_type=jnp.float32)
-        s = jnp.where(visible, s, -jnp.inf)
+        s = jnp.where(visible(), s, -jnp.inf)
         m_old = m_run[g]
         m_new = jnp.maximum(m_old, jnp.max(s, axis=0, keepdims=True))
         alpha = jnp.exp2((m_old - m_new) * scale2)
         p = jnp.exp2(s * scale2 - m_new * scale2)
         total = jnp.sum(l_run[g] * alpha, axis=0, keepdims=True) + jnp.sum(p, axis=0, keepdims=True)
-        fresh = lax.dot_general(newvt[...], p.astype(jnp.bfloat16), (((0,), (0,)), ((), ())),
+        fresh = lax.dot_general(newv[...], p.astype(jnp.bfloat16), (((0,), (0,)), ((), ())),
                                 preferred_element_type=jnp.float32)
         out = ((acc[g] * alpha + fresh) / total).T.astype(jnp.bfloat16)
-        for s_i in range(CHIPS):
-            o_send[s_i, :, g * HEAD:(g + 1) * HEAD] = out[s_i * tok:(s_i + 1) * tok, :]
-
-    wide_cols = GROUP * HEAD
-    here = pl.ds(pl.multiple_of(chip * wide_cols, HEAD), wide_cols)
-    o_copies = [remote(o_send.at[s], o_all.at[:, here], o_ssem.at[s - 1], o_rsem.at[s - 1], across[s]) for s in range(1, CHIPS)]
-    for c in o_copies:
-        c.start()
-    o_all[:, here] = o_send[0]
+        for s_i in range(1, CHIPS):
+            o_send[g, s_i] = out[s_i * tok:(s_i + 1) * tok, :]
+            o_copy(g, s_i).start()
+        o_all[:, pl.ds(pl.multiple_of(chip * wide_cols + g * HEAD, HEAD), HEAD)] = out[:tok, :]
+
+    def step(item, carry):
+        nxt = item + 1
+        early = (nxt < n_first) & (nxt % GROUP == 0)
+
+        @pl.when(early | (nxt == n_first) | (nxt == n_first + 1))
+        def _():
+            ready(place(nxt)[0])
+
+        @pl.when(item == n_first)
+        def _():
+            for c in new_copies:
+                c.wait_recv()
+            for s in range(CHIPS):
+                at = (CHIPS + s) * tok
+                newk[at:at + tok, :] = peer_new[s, 0]
+                newv[at:at + tok, :] = peer_new[s, 1]
+
+        after = jnp.minimum(nxt, n_items - 1)
+
+        @pl.when(item % 2 == 0)
+        def _():
+            score(after, s_odd, m_odd)
+            absorb(item, s_even, m_even)
+
+        @pl.when(item % 2 == 1)
+        def _():
+            score(after, s_even, m_even)
+            absorb(item, s_odd, m_odd)
+
+        @pl.when((item > n_first) & ((item - n_first) % 2 == 1))
+        def _():
+            finish((item - n_first) // 2)
+
+        return carry
+
+    lax.fori_loop(0, n_items, step, 0)
+    o_copies = [o_copy(g, s) for g in range(GROUP) for s in range(1, CHIPS)]
     wo_load.wait()
     for c in o_copies:
         c.wait_recv()
@@ -309,7 +330,7 @@
                     kv_copy(step, which).wait_send()
 
 
-def run_layer(a, bias, cos_t, sin_t, k4, v4, k_in, v_in, w_q, w_k, w_v, w_o, collective_id):
+def run_layer(a, bias, trig, k4, v4, k_in, v_in, w_q, w_k, w_v, w_o, collective_id):
     resharded = k_in is not None
     tok, width = a.shape
     chunk = k4.shape[1]
@@ -324,11 +345,12 @@
         out_shape=[jax.ShapeDtypeStruct((tok, width), bf16),
                    jax.ShapeDtypeStruct((KV_HEADS, tok, HEAD), bf16),
                    jax.ShapeDtypeStruct((KV_HEADS, tok, HEAD), bf16)],
-        in_specs=[vmem] * 4 + [hbm] * (len(caches) + 4),
+        in_specs=[vmem] * 2 + [hbm] * (len(caches) + 5),
         out_specs=[vmem] * 3,
         scratch_shapes=[
             pltpu.VMEM((tok, width), bf16),
-            pltpu.VMEM((4, width, COL), bf16),
+            pltpu.VMEM((tok, 2 * HEAD), f32),
+            pltpu.VMEM((2,) + w_k.shape, bf16),
             pltpu.VMEM(w_o.shape, bf16),
             pltpu.VMEM((SLOTS, chunk, HEAD), bf16),
             pltpu.VMEM((SLOTS, chunk, HEAD), bf16),
@@ -346,16 +368,16 @@
             pltpu.VMEM((GROUP, HEAD, rows), f32),
             pltpu.VMEM((GROUP, 1, rows), f32),
             pltpu.VMEM((GROUP, 8, rows), f32),
-            pltpu.VMEM((CHIPS, tok, GROUP * HEAD), bf16),
+            pltpu.VMEM((GROUP, CHIPS, tok, HEAD), bf16),
             pltpu.VMEM((tok, CHIPS * GROUP * HEAD), bf16),
-            dma((4,)), dma, dma((2 * SLOTS,)),
+            dma, dma((2 + CHIPS,)), dma, dma((2 * SLOTS,)),
             dma((CHIPS - 1, 2)), dma((CHIPS - 1, 2)), dma((CHIPS, 2)), dma((CHIPS, 2)),
             dma((CHIPS - 1,)), dma((CHIPS - 1,)), dma((CHIPS,)), dma((CHIPS,)),
-            dma((CHIPS - 1,)), dma((CHIPS - 1,)),
+            dma((GROUP, CHIPS - 1)), dma((GROUP, CHIPS - 1)),
         ],
         compiler_params=pltpu.CompilerParams(collective_id=collective_id, has_side_effects=True, vmem_limit_bytes=60 * MIB),
         name="layer",
-    )(a, bias, cos_t, sin_t, *caches, w_q, w_k, w_v, w_o)
+    )(a, bias, trig, *caches, w_q, w_k, w_v, w_o)
 
 
 def mlp_kernel(h_ref, k4_ref, v4_ref, gate_ref, up_ref, down_ref, g_ref, kout_ref, vout_ref,
@@ -475,9 +497,22 @@
     return lax.optimization_barrier(jnp.transpose(cache, (1, 0, 2)))
 
 
-def pack_bias(b_q, b_k):
-    wide = jnp.concatenate([b_q.astype(jnp.float32), b_k.astype(jnp.float32), jnp.zeros(b_k.shape, jnp.float32)])
-    return wide.reshape(-1, 1, COL)
+def order_kernel(g_ref, y_ref, *refs):
+    g_out, y_out = refs[4:6]
+    g_out[...] = g_ref[...]
+    y_out[...] = y_ref[...]
+    for src, dst in zip(refs[:4], refs[6:]):
+        for c in range(KV_HEADS):
+            dst[:, c, :] = src[c]
+
+
+def order_outputs(hidden, y_two, *appends):
+    tok = hidden.shape[0]
+    rows = [jax.ShapeDtypeStruct(t.shape, t.dtype) for t in (hidden, y_two)]
+    lines = [jax.ShapeDtypeStruct((tok, KV_HEADS, HEAD), t.dtype) for t in appends]
+    vmem = pl.BlockSpec(memory_space=pltpu.VMEM)
+    return pl.pallas_call(order_kernel, out_shape=rows + lines, in_specs=[vmem] * 6, out_specs=[vmem] * 6,
+                          name="order_outputs")(hidden, y_two, *appends)
 
 
 def solution(mesh):
@@ -491,18 +526,14 @@
     out_specs = (rows_spec, rows_spec, cache_spec, cache_spec, cache_spec, cache_spec)
 
     def forward(x_in, cache_k1, cache_v1, w_q1, b_q1, w_k1, b_k1, w_v1, w_o1, w_gate, w_up, w_down, cache_k2, cache_v2, w_q2, b_q2, w_k2, b_k2, w_v2, w_o2):
-        me = lax.axis_index('cp')
-        tok = x_in.shape[0]
-        positions = axis_size * cache_k1.shape[0] + me * tok + jnp.arange(tok)
-        cos_t, sin_t = rope_tables(positions)
+        n_tok = axis_size * x_in.shape[0]
+        trig = rope_table(axis_size * cache_k1.shape[0], n_tok)
+        bias = jnp.concatenate([b_q1, b_k1, b_q2, b_k2]).astype(jnp.float32).reshape(1, -1)
         k4a, v4a = heads_first(cache_k1), heads_first(cache_v1)
         k4b, v4b = heads_first(cache_k2), heads_first(cache_v2)
-        resid_h, k_one, v_one = run_layer(x_in, pack_bias(b_q1, b_k1), cos_t, sin_t, k4a, v4a, None, None,
-                                          w_q1, w_k1, w_v1, w_o1, 1)
+        resid_h, k_one, v_one = run_layer(x_in, bias, trig, k4a, v4a, None, None, w_q1, w_k1, w_v1, w_o1, 1)
         hidden, k_in, v_in = run_mlp(resid_h, k4b, v4b, w_gate, w_up, w_down, 2)
-        y_two, k_two, v_two = run_layer(hidden, pack_bias(b_q2, b_k2), cos_t, sin_t, k4b, v4b, k_in, v_in,
-                                        w_q2, w_k2, w_v2, w_o2, 3)
-        back = lambda t: jnp.transpose(t, (1, 0, 2))
-        return hidden, y_two, back(k_one), back(v_one), back(k_two), back(v_two)
+        y_two, k_two, v_two = run_layer(hidden, bias, trig, k4b, v4b, k_in, v_in, w_q2, w_k2, w_v2, w_o2, 3)
+        return order_outputs(hidden, y_two, k_one, v_one, k_two, v_two)
 
     return jax.shard_map(forward, mesh=mesh, in_specs=in_specs, out_specs=out_specs, check_vma=False)

time: 262 us -> 244 us (0.931)
  Pallas kernels: 239 us -> 231 us
  local copies, waits for them, and re-layouts: 18.1 us -> 11.6 us
  other arithmetic: 3.84 us -> 0.65 us
    pallas_call x2, Pallas kernels: 172 us -> 162 us  [run_layer(): pl.pallas_call(functools.partial(layer_kernel, resharded), out_shape=[jax...]
    unnamed x18 -> x10, local copies, waits for them, and re-layouts: 16.9 us -> 8.71 us
    concatenate x0 -> x4, local copies, waits for them, and re-layouts: none -> 2.93 us  [forward(): jnp.concatenate([b_q1, b_k1, b_q2, b_k2]).astype(jnp.float32).reshape(1, -1)]
    pallas_call x0 -> x1, Pallas kernels: none -> 2.66 us  [order_outputs(): pl.pallas_call(order_kernel, out_shape=rows + lines, in_specs=[vmem] * 6,...]
where the time goes in v2:
time: 244 us
  Pallas kernels  231 us (95%)
  local copies, waits for them, and re-layouts  11.6 us (5%)
    pallas_call x2, Pallas kernels, run_layer(): pl.pallas_call(functools.partial(layer_kernel, resharded), out_shape=[jax...  162 us
    pallas_call x1, Pallas kernels, run_mlp(): pl.pallas_call(mlp_kernel, out_shape=[jax.ShapeDtypeStruct((tok, width),...  66.5 us
    unnamed x10, local copies, waits for them, and re-layouts  8.71 us

profile of v2, /device:TPU:0, one launch (start us, length us, event | category | flops | bytes accessed | tf_op | source)
XLA Modules:
  0.0 243.9 jit_solution(213085490716215845)
XLA Ops:
  0.6 0.0 copy-start
  0.6 0.8 concatenate.19
  1.5 0.7 concatenate.21
  2.2 0.7 concatenate.18
  2.9 0.7 concatenate.20
  3.6 0.7 maximum_convert_fusion.bias_ref
  4.2 3.2 %copy.38 = bf16[2048,4,128]{2,0,1:T(8,128)(2,1)} copy(bf16[2048,4,128]{2,1,0:T(4,128)(2,1)} %param.22) | data formatting | bytes 4194304 | tf_op args[1]
  7.4 0.0 copy-done
  7.4 1.6 copy.37
  9.0 0.0 copy-start.1
  9.0 85.1 %layer.2 = (bf16[64,3584]{1,0:T(8,128)(2,1)}, bf16[4,64,128]{2,1,0:T(8,128)(2,1)}, bf16[4,64,128]{2,1,0:T(8,128)(2,1)}) custom-call(bf16[64,3584]{1,0:T(8,128)(2,1)} %a_ref.1, f32[1,8192]{1,0:T(1,128)} %maximum_convert_fusion.bias_ref, f32[512,256]{1,0:T(8,128)} %constant.2.clone.trig_ref, bf16[4,2048,128]{2,1,0:T(8,128)(2,1)} %bitcast.16, ...), custom_call_target="tpu_custom_call" | custom-call | tf_op jit(solution)/shard_map/layer/pallas_call | solution.py:343
  94.1 0.0 copy-start.2
  94.1 0.0 copy-done.1
  94.1 1.6 copy.36
  95.8 0.7 copy-done.2
  96.5 1.6 copy.35
  98.0 66.5 %mlp.1 = (bf16[64,3584]{1,0:T(8,128)(2,1)}, bf16[8,2048,128]{2,1,0:T(8,128)(2,1)}, bf16[8,2048,128]{2,1,0:T(8,128)(2,1)}) custom-call(bf16[64,3584]{1,0:T(8,128)(2,1)} %get-tuple-element.15.h_ref, bf16[4,2048,128]{2,1,0:T(8,128)(2,1)} %bitcast.12, bf16[4,2048,128]{2,1,0:T(8,128)(2,1)} %bitcast.14, bf16[3584,18944]{1,0:T(8,128)(2,1)} %gate_ref.1, ...), custom_call_target="tpu_custom_call" | custom-call | tf_op jit(solution)/shard_map/mlp/pallas_call | solution.py:476
  164.5 76.7 %layer.3 = (bf16[64,3584]{1,0:T(8,128)(2,1)}, bf16[4,64,128]{2,1,0:T(8,128)(2,1)}, bf16[4,64,128]{2,1,0:T(8,128)(2,1)}) custom-call(bf16[64,3584]{1,0:T(8,128)(2,1)} %get-tuple-element.16.a_ref.g_ref, f32[1,8192]{1,0:T(1,128)} %maximum_convert_fusion.bias_ref, f32[512,256]{1,0:T(8,128)} %constant.2.clone.trig_ref, bf16[4,2048,128]{2,1,0:T(8,128)(2,1)} %bitcast.13, ...), custom_call_target="tpu_custom_call" | custom-call | tf_op jit(solution)/shard_map/layer/pallas_call | solution.py:343
  241.2 2.7 %order_outputs.1 = (bf16[64,3584]{1,0:T(8,128)(2,1)}, bf16[64,3584]{1,0:T(8,128)(2,1)}, bf16[64,4,128]{2,1,0:T(4,128)(2,1)}, bf16[64,4,128]{2,1,0:T(4,128)(2,1)}...) custom-call(bf16[64,3584]{1,0:T(8,128)(2,1)} %get-tuple-element.16.a_ref.g_ref, ...), custom_call_target="tpu_custom_call" | custom-call | tf_op jit(solution)/shard_map/order_outputs/pallas_call | solution.py:514
Async XLA Ops:
  0.6 6.8 %copy-start = (bf16[2048,4,128]{2,1,0:T(4,128)(2,1)S(1)}, bf16[2048,4,128]{2,1,0:T(4,128)(2,1)}, u32[]{:S(2)}) copy-start(bf16[2048,4,128]{2,1,0:T(4,128)(2,1)} %param.23) | copy-start | bytes 6291460
  9.0 85.1 %copy-start.1 = (bf16[2048,4,128]{2,1,0:T(4,128)(2,1)S(1)}, bf16[2048,4,128]{2,1,0:T(4,128)(2,1)}, u32[]{:S(2)}) copy-start(bf16[2048,4,128]{2,1,0:T(4,128)(2,1)} %param.33) | copy-start | bytes 6291460
  94.1 2.4 copy-start.2

commit v3 on v2

--- a/solution.py
+++ b/solution.py
@@ -62,7 +62,7 @@
         wq_ref, wk_ref, wv_ref, wo_ref = refs[:4]
         refs = refs[4:]
     (y_ref, knew_ref, vnew_ref, xn, trig, wkv, wo, kb, vb, vt, msg, got, peer_new, newk, newv, qt,
-     s_even, s_odd, m_even, m_odd, acc, m_run, l_run, o_send, o_all,
+     s_even, s_odd, m_even, m_odd, acc, m_run, l_run, hide, o_send, o_all,
      trig_sem, w_sem, wo_sem, loc_sem, kv_send, kv_recv, pair_send, pair_recv, q_send, q_recv,
      new_send, new_recv, o_ssem, o_rsem) = refs
     chip, core, across, partner = peers()
@@ -73,8 +73,8 @@
     rows = qt.shape[2]
     wide_cols = GROUP * HEAD
     n_q = wq_ref.shape[1]
-    n_items = SLOTS * GROUP
-    n_first = (SLOTS - 2) * GROUP
+    n_items = CHIPS * GROUP
+    n_first = (CHIPS - 1) * GROUP
     bias_at = (n_q + wk_ref.shape[1]) if resharded else 0
 
     def wq_copy(n):
@@ -111,6 +111,9 @@
         for j in range(1, SLOTS):
             loads.append((pltpu.make_async_copy(kin_ref.at[j], kb.at[j], loc_sem.at[2 * j]),
                           pltpu.make_async_copy(vin_ref.at[j], vb.at[j], loc_sem.at[2 * j + 1])))
+        for pair in loads:
+            for c in pair:
+                c.start()
     else:
         for which in range(2):
             pair_copy(0, which).start()
@@ -130,7 +133,7 @@
 
     kv_loads[0].wait()
     k_pre = (jnp.dot(xn[...], wkv[0], preferred_element_type=jnp.float32)
-             + bias_ref[:, bias_at + n_q:bias_at + n_q + KV_HEADS * HEAD]).astype(jnp.bfloat16)
+             + bias_ref[:, bias_at + n_q:bias_at + n_q + KV_HEADS * HEAD].astype(jnp.float32)).astype(jnp.bfloat16)
     for c in range(KV_HEADS):
         knew_ref[c] = rope(k_pre[:, c * HEAD:(c + 1) * HEAD])
     kv_loads[1].wait()
@@ -145,7 +148,7 @@
         pltpu.make_async_copy(wo.at[:, :wide_cols], wo.at[:, :wide_cols], w_sem.at[2 + n]).wait()
         grp = chip ^ (CHIPS - 1 - n)
         cols = pl.ds(pl.multiple_of(n * wide_cols, HEAD), wide_cols)
-        bias = bias_ref[:, pl.ds(pl.multiple_of(bias_at + grp * wide_cols, HEAD), wide_cols)]
+        bias = bias_ref[:, pl.ds(pl.multiple_of(bias_at + grp * wide_cols, HEAD), wide_cols)].astype(jnp.float32)
         q_pre = (jnp.dot(xn[...], wo[:, cols], preferred_element_type=jnp.float32) + bias).astype(jnp.bfloat16)
         for g in range(GROUP):
             msg[n, g] = rope(q_pre[:, g * HEAD:(g + 1) * HEAD])
@@ -162,11 +165,7 @@
     q_copies = [q_copy(n) for n in range(CHIPS - 1)]
     parts = [msg.at[CHIPS - 1]] + [got.at[CHIPS - 1 - s] for s in range(1, CHIPS)]
     wo_load = pltpu.make_async_copy(wo_ref, wo, wo_sem)
-    if resharded:
-        for pair in loads:
-            for c in pair:
-                c.start()
-    else:
+    if not resharded:
         for step, which in ((1, 1), (2, 1), (3, 0), (3, 1)):
             kv_copy(step, which).start()
     wo_load.start()
@@ -185,35 +184,40 @@
         newv[s * tok:(s + 1) * tok, :] = parts[s][GROUP + 1]
 
     def ready(j):
-        for jj in range(SLOTS):
+        for jj in range(CHIPS):
             @pl.when(j == jj)
             def _():
                 if jj == 0:
                     for c in own:
                         c.wait()
                 elif resharded:
-                    for c in loads[jj - 1]:
+                    for c in loads[2 * jj - 1]:
                         c.wait()
-                elif jj % 2 == 0:
-                    for which in range(2):
-                        kv_copy(jj // 2, which).wait_recv()
-                        pair_copy(jj // 2, which).start()
                 else:
                     for which in range(2):
-                        pair_copy(jj // 2, which).wait_recv()
-
-        vt[j % 2] = vb[j].T
+                        kv_copy(jj, which).wait_recv()
+                        pair_copy(jj, which).start()
+        vt[j % 2, :, :chunk] = vb[2 * j].T
+        for jj in range(CHIPS):
+            @pl.when(j == jj)
+            def _():
+                if resharded:
+                    for c in loads[2 * jj]:
+                        c.wait()
+                else:
+                    for which in range(2):
+                        pair_copy(jj, which).wait_recv()
+        vt[j % 2, :, chunk:] = vb[2 * j + 1].T
 
     def place(item):
-        late = item - n_first
-        is_late = late >= 0
-        return jnp.where(is_late, SLOTS - 2 + late % 2, item // GROUP), jnp.where(is_late, late // 2, item % GROUP)
+        return item // GROUP, item % GROUP
 
     def score(item, s_dst, m_dst):
         j, g = place(item)
         part = jnp.full((8, rows), -jnp.inf, jnp.float32)
-        for t in range(chunk // 256):
-            s_blk = jnp.dot(kb[j, t * 256:(t + 1) * 256, :], qt[g], preferred_element_type=jnp.float32)
+        for t in range(2 * chunk // 256):
+            at = (t * 256) % chunk
+            s_blk = jnp.dot(kb[2 * j + t * 256 // chunk, at:at + 256, :], qt[g], preferred_element_type=jnp.float32)
             s_dst[t * 256:(t + 1) * 256, :] = s_blk
             part = jnp.maximum(part, jnp.max(s_blk.reshape(32, 8, rows), axis=0))
         m_dst[...] = part
@@ -226,7 +230,7 @@
         shift = m_new * scale2
         l_part = jnp.zeros((8, rows), jnp.float32)
         out = jnp.zeros((HEAD, rows), jnp.float32)
-        for t in range(chunk // 256):
+        for t in range(2 * chunk // 256):
             p = jnp.exp2(s_src[t * 256:(t + 1) * 256, :] * scale2 - shift)
             l_part = l_part + jnp.sum(p.reshape(32, 8, rows), axis=0)
             out = out + jnp.dot(vt[j % 2, :, t * 256:(t + 1) * 256], p.astype(jnp.bfloat16),
@@ -240,13 +244,12 @@
 
     new_len = newk.shape[0]
 
-    def visible():
-        key_i = lax.broadcasted_iota(jnp.int32, (new_len, rows), 0)
-        qry_i = lax.broadcasted_iota(jnp.int32, (new_len, rows), 1)
-        blk = key_i // tok
-        k_pos = (2 * (chip ^ (blk % CHIPS)) + (core ^ (blk // CHIPS))) * tok + key_i % tok
-        q_pos = (2 * (chip ^ (qry_i // tok)) + core) * tok + qry_i % tok
-        return k_pos <= q_pos
+    key_i = lax.broadcasted_iota(jnp.int32, (new_len, rows), 0)
+    qry_i = lax.broadcasted_iota(jnp.int32, (new_len, rows), 1)
+    blk = key_i // tok
+    k_pos = (2 * (chip ^ (blk % CHIPS)) + (core ^ (blk // CHIPS))) * tok + key_i % tok
+    q_pos = (2 * (chip ^ (qry_i // tok)) + core) * tok + qry_i % tok
+    hide[...] = jnp.where(k_pos <= q_pos, 0.0, -jnp.inf)
 
     def o_copy(g, s):
         src = o_send.at[g, s]
@@ -254,8 +257,7 @@
         return remote(src, dst, o_ssem.at[g, s - 1], o_rsem.at[g, s - 1], across[s])
 
     def finish(g):
-        s = jnp.dot(newk[...], qt[g], preferred_element_type=jnp.float32)
-        s = jnp.where(visible(), s, -jnp.inf)
+        s = jnp.dot(newk[...], qt[g], preferred_element_type=jnp.float32) + hide[...]
         m_old = m_run[g]
         m_new = jnp.maximum(m_old, jnp.max(s, axis=0, keepdims=True))
         alpha = jnp.exp2((m_old - m_new) * scale2)
@@ -271,11 +273,10 @@
 
     def step(item, carry):
         nxt = item + 1
-        early = (nxt < n_first) & (nxt % GROUP == 0)
-
-        @pl.when(early | (nxt == n_first) | (nxt == n_first + 1))
-        def _():
-            ready(place(nxt)[0])
+
+        @pl.when((nxt % GROUP == 0) & (nxt < n_items))
+        def _():
+            ready(nxt // GROUP)
 
         @pl.when(item == n_first)
         def _():
@@ -298,9 +299,9 @@
             score(after, s_even, m_even)
             absorb(item, s_odd, m_odd)
 
-        @pl.when((item > n_first) & ((item - n_first) % 2 == 1))
-        def _():
-            finish((item - n_first) // 2)
+        @pl.when(item >= n_first)
+        def _():
+            finish(item - n_first)
 
         return carry
 
@@ -354,20 +355,21 @@
             pltpu.VMEM(w_o.shape, bf16),
             pltpu.VMEM((SLOTS, chunk, HEAD), bf16),
             pltpu.VMEM((SLOTS, chunk, HEAD), bf16),
-            pltpu.VMEM((2, HEAD, chunk), bf16),
+            pltpu.VMEM((2, HEAD, 2 * chunk), bf16),
             pltpu.VMEM((KV_HEADS, GROUP + 2, tok, HEAD), bf16),
             pltpu.VMEM((CHIPS - 1, GROUP + 2, tok, HEAD), bf16),
             pltpu.VMEM((CHIPS, 2, tok, HEAD), bf16),
             pltpu.VMEM((2 * rows, HEAD), bf16),
             pltpu.VMEM((2 * rows, HEAD), bf16),
             pltpu.VMEM((GROUP, HEAD, rows), bf16),
-            pltpu.VMEM((chunk, rows), f32),
-            pltpu.VMEM((chunk, rows), f32),
+            pltpu.VMEM((2 * chunk, rows), f32),
+            pltpu.VMEM((2 * chunk, rows), f32),
             pltpu.VMEM((8, rows), f32),
             pltpu.VMEM((8, rows), f32),
             pltpu.VMEM((GROUP, HEAD, rows), f32),
             pltpu.VMEM((GROUP, 1, rows), f32),
             pltpu.VMEM((GROUP, 8, rows), f32),
+            pltpu.VMEM((2 * rows, rows), f32),
             pltpu.VMEM((GROUP, CHIPS, tok, HEAD), bf16),
             pltpu.VMEM((tok, CHIPS * GROUP * HEAD), bf16),
             dma, dma((2 + CHIPS,)), dma, dma((2 * SLOTS,)),
@@ -528,7 +530,7 @@
     def forward(x_in, cache_k1, cache_v1, w_q1, b_q1, w_k1, b_k1, w_v1, w_o1, w_gate, w_up, w_down, cache_k2, cache_v2, w_q2, b_q2, w_k2, b_k2, w_v2, w_o2):
         n_tok = axis_size * x_in.shape[0]
         trig = rope_table(axis_size * cache_k1.shape[0], n_tok)
-        bias = jnp.concatenate([b_q1, b_k1, b_q2, b_k2]).astype(jnp.float32).reshape(1, -1)
+        bias = jnp.concatenate([b_q1, b_k1, b_q2, b_k2]).reshape(1, -1)
         k4a, v4a = heads_first(cache_k1), heads_first(cache_v1)
         k4b, v4b = heads_first(cache_k2), heads_first(cache_v2)
         resid_h, k_one, v_one = run_layer(x_in, bias, trig, k4a, v4a, None, None, w_q1, w_k1, w_v1, w_o1, 1)

time: 244 us -> 237 us (0.971)
  Pallas kernels: 231 us -> 225 us
    pallas_call x2, Pallas kernels: 162 us -> 156 us  [run_layer(): pl.pallas_call(functools.partial(layer_kernel, resharded), out_shape=[jax...]
    concatenate x4 -> x0, local copies, waits for them, and re-layouts: 2.93 us -> none  [forward(): jnp.concatenate([b_q1, b_k1, b_q2, b_k2]).astype(jnp.float32).reshape(1, -1)]
where the time goes in v3:
time: 237 us; the launch traced here: 236 us
  Pallas kernels  225 us (95%)
  local copies, waits for them, and re-layouts  9.34 us (4%)
    pallas_call x2, Pallas kernels, run_layer(): pl.pallas_call(functools.partial(layer_kernel, resharded), out_shape=[jax...  156 us
    pallas_call x1, Pallas kernels, run_mlp(): pl.pallas_call(mlp_kernel, out_shape=[jax.ShapeDtypeStruct((tok, width),...  66.6 us
    unnamed x10, local copies, waits for them, and re-layouts  8.71 us

profile of v3, /device:TPU:0, one launch (start us, length us, event | category | flops | bytes accessed | tf_op | source)
XLA Modules:
  0.0 236.3 jit_solution(3137229848299208385)
XLA Ops:
  0.6 0.0 copy-start
  0.6 0.9 pad_maximum_fusion
  1.5 0.6 reshape.15.bias_ref
  2.2 3.2 %copy.38 = bf16[2048,4,128]{2,0,1:T(8,128)(2,1)} copy(bf16[2048,4,128]{2,1,0:T(4,128)(2,1)} %param.22) | data formatting | bytes 4194304 | tf_op args[1]
  5.4 0.0 copy-done
  5.4 1.6 copy.37
  7.0 0.0 copy-start.1
  7.0 84.1 %layer.2 = (bf16[64,3584]{1,0:T(8,128)(2,1)}, bf16[4,64,128]{2,1,0:T(8,128)(2,1)}, bf16[4,64,128]{2,1,0:T(8,128)(2,1)}) custom-call(bf16[64,3584]{1,0:T(8,128)(2,1)} %a_ref.1, bf16[1,8192]{1,0:T(2,128)(2,1)} %reshape.15.bias_ref, f32[512,256]{1,0:T(8,128)} %constant.2.clone.trig_ref, bf16[4,2048,128]{2,1,0:T(8,128)(2,1)} %bitcast.16, ...), custom_call_target="tpu_custom_call" | custom-call | tf_op jit(solution)/shard_map/layer/pallas_call | solution.py:344
  91.1 0.0 copy-start.2
  91.1 0.0 copy-done.1
  91.1 1.6 copy.36
  92.7 0.7 copy-done.2
  93.4 1.6 copy.35
  95.0 66.6 %mlp.1 = (bf16[64,3584]{1,0:T(8,128)(2,1)}, bf16[8,2048,128]{2,1,0:T(8,128)(2,1)}, bf16[8,2048,128]{2,1,0:T(8,128)(2,1)}) custom-call(bf16[64,3584]{1,0:T(8,128)(2,1)} %get-tuple-element.15.h_ref, bf16[4,2048,128]{2,1,0:T(8,128)(2,1)} %bitcast.12, bf16[4,2048,128]{2,1,0:T(8,128)(2,1)} %bitcast.14, bf16[3584,18944]{1,0:T(8,128)(2,1)} %gate_ref.1, ...), custom_call_target="tpu_custom_call" | custom-call | tf_op jit(solution)/shard_map/mlp/pallas_call | solution.py:478
  161.7 71.9 %layer.3 = (bf16[64,3584]{1,0:T(8,128)(2,1)}, bf16[4,64,128]{2,1,0:T(8,128)(2,1)}, bf16[4,64,128]{2,1,0:T(8,128)(2,1)}) custom-call(bf16[64,3584]{1,0:T(8,128)(2,1)} %get-tuple-element.16.a_ref.g_ref, bf16[1,8192]{1,0:T(2,128)(2,1)} %reshape.15.bias_ref, f32[512,256]{1,0:T(8,128)} %constant.2.clone.trig_ref, bf16[4,2048,128]{2,1,0:T(8,128)(2,1)} %bitcast.13, ...), custom_call_target="tpu_custom_call" | custom-call | tf_op jit(solution)/shard_map/layer/pallas_call | solution.py:344
  233.6 2.7 %order_outputs.1 = (bf16[64,3584]{1,0:T(8,128)(2,1)}, bf16[64,3584]{1,0:T(8,128)(2,1)}, bf16[64,4,128]{2,1,0:T(4,128)(2,1)}, bf16[64,4,128]{2,1,0:T(4,128)(2,1)}...) custom-call(bf16[64,3584]{1,0:T(8,128)(2,1)} %get-tuple-element.16.a_ref.g_ref, ...), custom_call_target="tpu_custom_call" | custom-call | tf_op jit(solution)/shard_map/order_outputs/pallas_call | solution.py:516
Async XLA Ops:
  0.6 4.8 %copy-start = (bf16[2048,4,128]{2,1,0:T(4,128)(2,1)S(1)}, bf16[2048,4,128]{2,1,0:T(4,128)(2,1)}, u32[]{:S(2)}) copy-start(bf16[2048,4,128]{2,1,0:T(4,128)(2,1)} %param.23) | copy-start | bytes 6291460
  7.0 84.1 %copy-start.1 = (bf16[2048,4,128]{2,1,0:T(4,128)(2,1)S(1)}, bf16[2048,4,128]{2,1,0:T(4,128)(2,1)}, u32[]{:S(2)}) copy-start(bf16[2048,4,128]{2,1,0:T(4,128)(2,1)} %param.33) | copy-start | bytes 6291460
  91.1 2.4 copy-start.2

commit v4 on v3

--- a/solution.py
+++ b/solution.py
@@ -18,6 +18,7 @@
 COL = 256
 SLOTS = 2 * CHIPS
 MIB = 1024 * 1024
+VMEM_ALL = 67_000_000
 MESH = pl.DeviceIdType.MESH
 
 
@@ -54,15 +55,43 @@
                                         device_id={'cp': dev}, device_id_type=MESH)
 
 
-def layer_kernel(resharded, a_ref, bias_ref, trig_ref, k4_ref, v4_ref, *refs):
-    if resharded:
-        kin_ref, vin_ref, wq_ref, wk_ref, wv_ref, wo_ref = refs[:6]
-        refs = refs[6:]
-    else:
-        wq_ref, wk_ref, wv_ref, wo_ref = refs[:4]
-        refs = refs[4:]
+PIECE = 256
+RING = 4
+
+
+def pack_start(src_ref, raw, sem):
+    for i in range(RING):
+        pltpu.make_async_copy(src_ref.at[pl.ds(i * PIECE, PIECE)], raw.at[i], sem.at[i]).start()
+
+
+def pack_heads(src_ref, raw, tmp, sem, put):
+    n = src_ref.shape[0] // PIECE
+
+    def piece(i, carry):
+        slot = i % RING
+        pltpu.make_async_copy(raw.at[slot], raw.at[slot], sem.at[slot]).wait()
+        for part in range(2):
+            half = PIECE // 2
+            flat = jnp.swapaxes(raw[slot, part * half:(part + 1) * half], 0, 1)
+            for c in range(KV_HEADS):
+                tmp[c, part * half:(part + 1) * half, :] = flat[c]
+
+        @pl.when(i + RING < n)
+        def _():
+            pltpu.make_async_copy(src_ref.at[pl.ds((i + RING) * PIECE, PIECE)], raw.at[slot], sem.at[slot]).start()
+
+        put(pl.ds(pl.multiple_of(i * PIECE, PIECE), PIECE))
+        return carry
+
+    lax.fori_loop(0, n, piece, 0)
+
+
+def layer_kernel(resharded, a_ref, bias_ref, trig_ref, kin_ref, vin_ref, wq_ref, wk_ref, wv_ref, wo_ref, *refs):
+    if not resharded:
+        raw_k, raw_v, tmp, k_out, v_out, raw_sem = refs[-6:]
+        refs = refs[:-6]
     (y_ref, knew_ref, vnew_ref, xn, trig, wkv, wo, kb, vb, vt, msg, got, peer_new, newk, newv, qt,
-     s_even, s_odd, m_even, m_odd, acc, m_run, l_run, hide, o_send, o_all,
+     s_even, s_odd, m_even, m_odd, acc, m_run, l_run, hide, o_send, o_all, y_acc,
      trig_sem, w_sem, wo_sem, loc_sem, kv_send, kv_recv, pair_send, pair_recv, q_send, q_recv,
      new_send, new_recv, o_ssem, o_rsem) = refs
     chip, core, across, partner = peers()
@@ -83,42 +112,50 @@
 
     kv_loads = [pltpu.make_async_copy(wk_ref, wkv.at[0], w_sem.at[0]), pltpu.make_async_copy(wv_ref, wkv.at[1], w_sem.at[1])]
     trig_load = pltpu.make_async_copy(trig_ref.at[pl.ds(me * tok, tok)], trig, trig_sem)
+    if not resharded:
+        pack_start(kin_ref, raw_k, raw_sem.at[0])
+        pack_start(vin_ref, raw_v, raw_sem.at[1])
     trig_load.start()
     for c in kv_loads + [wq_copy(n) for n in range(CHIPS)]:
         c.start()
     meet(across[1:] + [partner])
 
-    own = [pltpu.make_async_copy(k4_ref.at[chip], kb.at[0], loc_sem.at[0]),
-           pltpu.make_async_copy(v4_ref.at[chip], vb.at[0], loc_sem.at[1])]
-    for c in own:
-        c.start()
-
-    def kv_copy(step, which):
-        src, dst = (k4_ref, kb) if which == 0 else (v4_ref, vb)
-        return remote(src.at[chip ^ step], dst.at[2 * step], kv_send.at[step - 1, which], kv_recv.at[step - 1, which],
-                      across[step])
-
-    def pair_copy(step, which):
+    halves = [pl.ds(h * (chunk // 2), chunk // 2) for h in range(2)]
+
+    def kv_copy(step, which, h):
+        src, dst = (k_out, kb) if which == 0 else (v_out, vb)
+        return remote(src.at[step - 1, halves[h]], dst.at[2 * step, halves[h]], kv_send.at[step - 1, which, h],
+                      kv_recv.at[step - 1, which, h], across[step])
+
+    def pair_copy(step, which, h):
         dst = kb if which == 0 else vb
-        if step == 0:
-            src = (k4_ref if which == 0 else v4_ref).at[chip]
-        else:
-            src = dst.at[2 * step]
-        return remote(src, dst.at[2 * step + 1], pair_send.at[step, which], pair_recv.at[step, which], partner)
+        return remote(dst.at[2 * step, halves[h]], dst.at[2 * step + 1, halves[h]], pair_send.at[step, which, h],
+                      pair_recv.at[step, which, h], partner)
 
     if resharded:
         loads = []
-        for j in range(1, SLOTS):
+        for j in range(SLOTS):
             loads.append((pltpu.make_async_copy(kin_ref.at[j], kb.at[j], loc_sem.at[2 * j]),
                           pltpu.make_async_copy(vin_ref.at[j], vb.at[j], loc_sem.at[2 * j + 1])))
         for pair in loads:
             for c in pair:
                 c.start()
     else:
+        def put(mine, out):
+            def store(span):
+                mine[0, span, :] = tmp[chip]
+                for step in range(1, CHIPS):
+                    out[step - 1, span, :] = tmp[chip ^ step]
+            return store
+
+        pack_heads(kin_ref, raw_k, tmp, raw_sem.at[0], put(kb, k_out))
+        for h in range(2):
+            for step in (1, 2):
+                kv_copy(step, 0, h).start()
+        pack_heads(vin_ref, raw_v, tmp, raw_sem.at[1], put(vb, v_out))
         for which in range(2):
-            pair_copy(0, which).start()
-        kv_copy(1, 0).start()
-        kv_copy(2, 0).start()
+            for h in range(2):
+                pair_copy(0, which, h).start()
 
     if resharded:
         xn[...] = norm_rows(a_ref[...].astype(jnp.float32))
@@ -166,8 +203,12 @@
     parts = [msg.at[CHIPS - 1]] + [got.at[CHIPS - 1 - s] for s in range(1, CHIPS)]
     wo_load = pltpu.make_async_copy(wo_ref, wo, wo_sem)
     if not resharded:
-        for step, which in ((1, 1), (2, 1), (3, 0), (3, 1)):
-            kv_copy(step, which).start()
+        for h in range(2):
+            for step in (1, 2):
+                kv_copy(step, 1, h).start()
+        for h in range(2):
+            for which in range(2):
+                kv_copy(3, which, h).start()
     wo_load.start()
     acc[...] = jnp.zeros_like(acc)
     m_run[...] = jnp.full_like(m_run, -jnp.inf)
@@ -187,26 +228,25 @@
         for jj in range(CHIPS):
             @pl.when(j == jj)
             def _():
-                if jj == 0:
-                    for c in own:
+                if resharded:
+                    for c in loads[2 * jj]:
                         c.wait()
-                elif resharded:
-                    for c in loads[2 * jj - 1]:
-                        c.wait()
-                else:
-                    for which in range(2):
-                        kv_copy(jj, which).wait_recv()
-                        pair_copy(jj, which).start()
+                elif jj:
+                    for h in range(2):
+                        for which in range(2):
+                            kv_copy(jj, which, h).wait_recv()
+                            pair_copy(jj, which, h).start()
         vt[j % 2, :, :chunk] = vb[2 * j].T
         for jj in range(CHIPS):
             @pl.when(j == jj)
             def _():
                 if resharded:
-                    for c in loads[2 * jj]:
+                    for c in loads[2 * jj + 1]:
                         c.wait()
                 else:
-                    for which in range(2):
-                        pair_copy(jj, which).wait_recv()
+                    for h in range(2):
+                        for which in range(2):
+                            pair_copy(jj, which, h).wait_recv()
         vt[j % 2, :, chunk:] = vb[2 * j + 1].T
 
     def place(item):
@@ -307,46 +347,75 @@
 
     lax.fori_loop(0, n_items, step, 0)
     o_copies = [o_copy(g, s) for g in range(GROUP) for s in range(1, CHIPS)]
+    last = 3 * (GROUP - 1)
     wo_load.wait()
-    for c in o_copies:
+    for c in o_copies[:last]:
         c.wait_recv()
 
+    def heads(s, first, count):
+        at = pl.multiple_of((chip ^ s) * wide_cols + first * HEAD, HEAD)
+        return pl.ds(at, count * HEAD)
+
+    def early_proj(blk, carry):
+        cols = pl.ds(pl.multiple_of(blk * COL, COL), COL)
+        total = jnp.zeros((tok, COL), jnp.float32)
+        for s in range(CHIPS):
+            part = heads(s, 0, GROUP if s == 0 else GROUP - 1)
+            total = total + jnp.dot(o_all[:, part], wo[part, cols], preferred_element_type=jnp.float32)
+        y_acc[:, cols] = total
+        return carry
+
+    lax.fori_loop(0, wo.shape[1] // COL, early_proj, 0)
+    for c in o_copies[last:]:
+        c.wait_recv()
+
     def out_proj(blk, carry):
-        cols = pl.ds(pl.multiple_of(blk * COL, COL), COL)
-        y = jnp.dot(o_all[...], wo[:, cols], preferred_element_type=jnp.float32).astype(jnp.bfloat16)
+        cols = pl.ds(pl.multiple_of(blk * 2 * COL, 2 * COL), 2 * COL)
+        total = y_acc[:, cols]
+        for s in range(1, CHIPS):
+            part = heads(s, GROUP - 1, 1)
+            total = total + jnp.dot(o_all[:, part], wo[part, cols], preferred_element_type=jnp.float32)
+        y = total.astype(jnp.bfloat16)
         if not resharded:
             y = (a_ref[:, cols].astype(jnp.float32) + y.astype(jnp.float32)).astype(jnp.bfloat16)
         y_ref[:, cols] = y
         return carry
 
-    lax.fori_loop(0, wo.shape[1] // COL, out_proj, 0)
+    lax.fori_loop(0, wo.shape[1] // (2 * COL), out_proj, 0)
 
     for c in q_copies + new_copies + o_copies:
         c.wait_send()
     if not resharded:
         for step in range(CHIPS):
             for which in range(2):
-                pair_copy(step, which).wait_send()
-                if step:
-                    kv_copy(step, which).wait_send()
-
-
-def run_layer(a, bias, trig, k4, v4, k_in, v_in, w_q, w_k, w_v, w_o, collective_id):
-    resharded = k_in is not None
+                for h in range(2):
+                    pair_copy(step, which, h).wait_send()
+                    if step:
+                        kv_copy(step, which, h).wait_send()
+
+
+def run_layer(resharded, a, bias, trig, k_in, v_in, w_q, w_k, w_v, w_o, collective_id):
     tok, width = a.shape
-    chunk = k4.shape[1]
+    chunk = k_in.shape[1] if resharded else k_in.shape[0]
     rows = CHIPS * tok
     bf16, f32 = jnp.bfloat16, jnp.float32
     vmem = pl.BlockSpec(memory_space=pltpu.VMEM)
     hbm = pl.BlockSpec(memory_space=pl.ANY)
     dma = pltpu.SemaphoreType.DMA
-    caches = (k4, v4, k_in, v_in) if resharded else (k4, v4)
+    packing = [] if resharded else [
+        pltpu.VMEM((RING, PIECE, KV_HEADS, HEAD), bf16),
+        pltpu.VMEM((RING, PIECE, KV_HEADS, HEAD), bf16),
+        pltpu.VMEM((KV_HEADS, PIECE, HEAD), bf16),
+        pltpu.VMEM((CHIPS - 1, chunk, HEAD), bf16),
+        pltpu.VMEM((CHIPS - 1, chunk, HEAD), bf16),
+        dma((2, RING)),
+    ]
     return pl.pallas_call(
         functools.partial(layer_kernel, resharded),
         out_shape=[jax.ShapeDtypeStruct((tok, width), bf16),
                    jax.ShapeDtypeStruct((KV_HEADS, tok, HEAD), bf16),
                    jax.ShapeDtypeStruct((KV_HEADS, tok, HEAD), bf16)],
-        in_specs=[vmem] * 2 + [hbm] * (len(caches) + 5),
+        in_specs=[vmem] * 2 + [hbm] * 7,
         out_specs=[vmem] * 3,
         scratch_shapes=[
             pltpu.VMEM((tok, width), bf16),
@@ -372,18 +441,20 @@
             pltpu.VMEM((2 * rows, rows), f32),
             pltpu.VMEM((GROUP, CHIPS, tok, HEAD), bf16),
             pltpu.VMEM((tok, CHIPS * GROUP * HEAD), bf16),
+            pltpu.VMEM((tok, width), f32),
             dma, dma((2 + CHIPS,)), dma, dma((2 * SLOTS,)),
-            dma((CHIPS - 1, 2)), dma((CHIPS - 1, 2)), dma((CHIPS, 2)), dma((CHIPS, 2)),
+            dma((CHIPS - 1, 2, 2)), dma((CHIPS - 1, 2, 2)), dma((CHIPS, 2, 2)), dma((CHIPS, 2, 2)),
             dma((CHIPS - 1,)), dma((CHIPS - 1,)), dma((CHIPS,)), dma((CHIPS,)),
             dma((GROUP, CHIPS - 1)), dma((GROUP, CHIPS - 1)),
-        ],
-        compiler_params=pltpu.CompilerParams(collective_id=collective_id, has_side_effects=True, vmem_limit_bytes=60 * MIB),
+        ] + packing,
+        compiler_params=pltpu.CompilerParams(collective_id=collective_id, has_side_effects=True, vmem_limit_bytes=VMEM_ALL),
         name="layer",
-    )(a, bias, trig, *caches, w_q, w_k, w_v, w_o)
-
-
-def mlp_kernel(h_ref, k4_ref, v4_ref, gate_ref, up_ref, down_ref, g_ref, kout_ref, vout_ref,
-               u, wg, wu, wd, acc, theirs, w_sem, u_send, u_recv, part_send, part_recv, kv_send, kv_recv, pair_send, pair_recv):
+    )(a, bias, trig, k_in, v_in, w_q, w_k, w_v, w_o)
+
+
+def mlp_kernel(h_ref, kin_ref, vin_ref, gate_ref, up_ref, down_ref, g_ref, kout_ref, vout_ref,
+               u, wg, wu, wd, acc, theirs, w_sem, u_send, u_recv, part_send, part_recv, kv_send, kv_recv, pair_send, pair_recv,
+               raw_k, raw_v, tmp, k_out, v_out, raw_sem, own_sem):
     chip, core, across, partner = peers()
     tok = h_ref.shape[0]
     n_buf = wg.shape[0]
@@ -396,6 +467,8 @@
                 pltpu.make_async_copy(up_ref.at[:, cols], wu.at[slot], w_sem.at[slot, 1]),
                 pltpu.make_async_copy(down_ref.at[cols, :], wd.at[slot], w_sem.at[slot, 2]))
 
+    pack_start(kin_ref, raw_k, raw_sem.at[0])
+    pack_start(vin_ref, raw_v, raw_sem.at[1])
     for b in range(n_buf):
         for c in copies(b):
             c.start()
@@ -405,21 +478,30 @@
     u_copy.start()
 
     def kv_copy(step, which):
-        src, dst = (k4_ref, kout_ref) if which == 0 else (v4_ref, vout_ref)
-        return remote(src.at[chip ^ step], dst.at[2 * step], kv_send.at[step - 1, which], kv_recv.at[step - 1, which],
+        src, dst = (k_out, kout_ref) if which == 0 else (v_out, vout_ref)
+        return remote(src.at[step], dst.at[2 * step], kv_send.at[step - 1, which], kv_recv.at[step - 1, which],
                       across[step])
 
     def pair_copy(step, which):
         dst = kout_ref if which == 0 else vout_ref
-        src = (k4_ref if which == 0 else v4_ref).at[chip] if step == 0 else dst.at[2 * step]
+        src = (k_out if which == 0 else v_out).at[0] if step == 0 else dst.at[2 * step]
         return remote(src, dst.at[2 * step + 1], pair_send.at[step, which], pair_recv.at[step, which], partner)
 
-    for step in range(1, CHIPS):
-        for which in range(2):
+    def put(out):
+        def store(span):
+            for step in range(CHIPS):
+                out[step, span, :] = tmp[chip ^ step]
+        return store
+
+    acc[...] = jnp.zeros_like(acc)
+    own = [pltpu.make_async_copy(k_out.at[0], kout_ref.at[0], own_sem.at[0]),
+           pltpu.make_async_copy(v_out.at[0], vout_ref.at[0], own_sem.at[1])]
+    for which, (src, raw, out) in enumerate(((kin_ref, raw_k, k_out), (vin_ref, raw_v, v_out))):
+        pack_heads(src, raw, tmp, raw_sem.at[which], put(out))
+        for step in range(1, CHIPS):
             kv_copy(step, which).start()
-    for which in range(2):
         pair_copy(0, which).start()
-    acc[...] = jnp.zeros_like(acc)
+        own[which].start()
     u_copy.wait_recv()
 
     def relay(step):
@@ -462,13 +544,15 @@
             pair_copy(step, which).wait()
             if step:
                 kv_copy(step, which).wait_send()
+    for c in own:
+        c.wait()
     u_copy.wait_send()
     part_copy.wait_send()
 
 
-def run_mlp(h, k4, v4, w_gate, w_up, w_down, collective_id):
+def run_mlp(h, cache_k, cache_v, w_gate, w_up, w_down, collective_id):
     tok, width = h.shape
-    chunk = k4.shape[1]
+    chunk = cache_k.shape[0]
     bf16, f32 = jnp.bfloat16, jnp.float32
     vmem = pl.BlockSpec(memory_space=pltpu.VMEM)
     hbm = pl.BlockSpec(memory_space=pl.ANY)
@@ -489,14 +573,16 @@
             pltpu.VMEM((tok, width), f32),
             dma((n_buf, 3)), dma, dma, dma, dma,
             dma((CHIPS - 1, 2)), dma((CHIPS - 1, 2)), dma((CHIPS, 2)), dma((CHIPS, 2)),
+            pltpu.VMEM((RING, PIECE, KV_HEADS, HEAD), bf16),
+            pltpu.VMEM((RING, PIECE, KV_HEADS, HEAD), bf16),
+            pltpu.VMEM((KV_HEADS, PIECE, HEAD), bf16),
+            pltpu.VMEM((CHIPS, chunk, HEAD), bf16),
+            pltpu.VMEM((CHIPS, chunk, HEAD), bf16),
+            dma((2, RING)), dma((2,)),
         ],
         compiler_params=pltpu.CompilerParams(collective_id=collective_id, has_side_effects=True, vmem_limit_bytes=60 * MIB),
         name="mlp",
-    )(h, k4, v4, w_gate, w_up, w_down)
-
-
-def heads_first(cache):
-    return lax.optimization_barrier(jnp.transpose(cache, (1, 0, 2)))
+    )(h, cache_k, cache_v, w_gate, w_up, w_down)
 
 
 def order_kernel(g_ref, y_ref, *refs):
@@ -531,11 +617,9 @@
         n_tok = axis_size * x_in.shape[0]
         trig = rope_table(axis_size * cache_k1.shape[0], n_tok)
         bias = jnp.concatenate([b_q1, b_k1, b_q2, b_k2]).reshape(1, -1)
-        k4a, v4a = heads_first(cache_k1), heads_first(cache_v1)
-        k4b, v4b = heads_first(cache_k2), heads_first(cache_v2)
-        resid_h, k_one, v_one = run_layer(x_in, bias, trig, k4a, v4a, None, None, w_q1, w_k1, w_v1, w_o1, 1)
-        hidden, k_in, v_in = run_mlp(resid_h, k4b, v4b, w_gate, w_up, w_down, 2)
-        y_two, k_two, v_two = run_layer(hidden, bias, trig, k4b, v4b, k_in, v_in, w_q2, w_k2, w_v2, w_o2, 3)
+        resid_h, k_one, v_one = run_layer(False, x_in, bias, trig, cache_k1, cache_v1, w_q1, w_k1, w_v1, w_o1, 1)
+        hidden, k_in, v_in = run_mlp(resid_h, cache_k2, cache_v2, w_gate, w_up, w_down, 2)
+        y_two, k_two, v_two = run_layer(True, hidden, bias, trig, k_in, v_in, w_q2, w_k2, w_v2, w_o2, 3)
         return order_outputs(hidden, y_two, k_one, v_one, k_two, v_two)
 
     return jax.shard_map(forward, mesh=mesh, in_specs=in_specs, out_specs=out_specs, check_vma=False)

time: 237 us -> 253 us (1.068)
  Pallas kernels: 225 us -> 251 us
  local copies, waits for them, and re-layouts: 9.34 us -> 0.63 us
    pallas_call x2, Pallas kernels: 156 us -> 176 us  [run_layer(): pl.pallas_call(functools.partial(layer_kernel, resharded), out_shape=[jax...]
    unnamed x10 -> x0, local copies, waits for them, and re-layouts: 8.71 us -> none
    pallas_call x1, Pallas kernels: 66.6 us -> 71.9 us  [run_mlp(): pl.pallas_call(mlp_kernel, out_shape=[jax.ShapeDtypeStruct((tok, width),...]
where the time goes in v4:
time: 253 us
  Pallas kernels  251 us (99%)
    pallas_call x2, Pallas kernels, run_layer(): pl.pallas_call(functools.partial(layer_kernel, resharded), out_shape=[jax...  176 us
    pallas_call x1, Pallas kernels, run_mlp(): pl.pallas_call(mlp_kernel, out_shape=[jax.ShapeDtypeStruct((tok, width),...  71.9 us

profile of v4, /device:TPU:0, one launch (start us, length us, event | category | flops | bytes accessed | tf_op | source)
XLA Modules:
  0.0 252.9 jit_solution(16401152506285774813)
XLA Ops:
  0.6 0.8 pad_maximum_fusion
  1.4 0.6 reshape.15.bias_ref
  2.0 104.6 %layer.2 = (bf16[64,3584]{1,0:T(8,128)(2,1)}, bf16[4,64,128]{2,1,0:T(8,128)(2,1)}, bf16[4,64,128]{2,1,0:T(8,128)(2,1)}) custom-call(bf16[64,3584]{1,0:T(8,128)(2,1)} %a_ref.1, bf16[1,8192]{1,0:T(2,128)(2,1)} %reshape.15.bias_ref, f32[512,256]{1,0:T(8,128)} %constant.2.clone.trig_ref, bf16[2048,4,128]{2,1,0:T(4,128)(2,1)} %kin_ref.2, ...), custom_call_target="tpu_custom_call" | custom-call | tf_op jit(solution)/shard_map/layer/pallas_call | solution.py:413
  106.7 71.9 %mlp.1 = (bf16[64,3584]{1,0:T(8,128)(2,1)}, bf16[8,2048,128]{2,1,0:T(8,128)(2,1)}, bf16[8,2048,128]{2,1,0:T(8,128)(2,1)}) custom-call(bf16[64,3584]{1,0:T(8,128)(2,1)} %get-tuple-element.15.h_ref, bf16[2048,4,128]{2,1,0:T(4,128)(2,1)} %kin_ref.3, bf16[2048,4,128]{2,1,0:T(4,128)(2,1)} %vin_ref.3, bf16[3584,18944]{1,0:T(8,128)(2,1)} %gate_ref.1, ...), custom_call_target="tpu_custom_call" | custom-call | tf_op jit(solution)/shard_map/mlp/pallas_call | solution.py:562
  178.6 71.7 %layer.3 = (bf16[64,3584]{1,0:T(8,128)(2,1)}, bf16[4,64,128]{2,1,0:T(8,128)(2,1)}, bf16[4,64,128]{2,1,0:T(8,128)(2,1)}) custom-call(bf16[64,3584]{1,0:T(8,128)(2,1)} %get-tuple-element.16.a_ref.g_ref, bf16[1,8192]{1,0:T(2,128)(2,1)} %reshape.15.bias_ref, f32[512,256]{1,0:T(8,128)} %constant.2.clone.trig_ref, ...), custom_call_target="tpu_custom_call" | custom-call | tf_op jit(solution)/shard_map/layer/pallas_call | solution.py:413
  250.2 2.7 %order_outputs.1 = (bf16[64,3584]{1,0:T(8,128)(2,1)}, bf16[64,3584]{1,0:T(8,128)(2,1)}, bf16[64,4,128]{2,1,0:T(4,128)(2,1)}, bf16[64,4,128]{2,1,0:T(4,128)(2,1)}...) custom-call(bf16[64,3584]{1,0:T(8,128)(2,1)} %get-tuple-element.16.a_ref.g_ref, ...), custom_call_target="tpu_custom_call" | custom-call | tf_op jit(solution)/shard_map/order_outputs/pallas_call | solution.py:602

commit v5 on v3

--- a/solution.py
+++ b/solution.py
@@ -18,6 +18,9 @@
 COL = 256
 SLOTS = 2 * CHIPS
 MIB = 1024 * 1024
+VMEM_ALL = 67_000_000
+PIECE = 256
+RING = 4
 MESH = pl.DeviceIdType.MESH
 
 
@@ -54,15 +57,57 @@
                                         device_id={'cp': dev}, device_id_type=MESH)
 
 
+def pack_start(src_ref, raw, sem):
+    for i in range(RING):
+        pltpu.make_async_copy(src_ref.at[pl.ds(i * PIECE, PIECE)], raw.at[i], sem.at[i]).start()
+
+
+def pack_heads(src_ref, dst_ref, raw, tmp, sem, out_sem):
+    n = src_ref.shape[0] // PIECE
+
+    def put(i, slot):
+        span = pl.ds(pl.multiple_of(i * PIECE, PIECE), PIECE)
+        return pltpu.make_async_copy(tmp.at[slot], dst_ref.at[:, span], out_sem.at[slot])
+
+    def piece(i, carry):
+        slot = i % RING
+        side = i % 2
+        pltpu.make_async_copy(raw.at[slot], raw.at[slot], sem.at[slot]).wait()
+
+        @pl.when(i >= 2)
+        def _():
+            put(i - 2, side).wait()
+
+        for part in range(2):
+            half = PIECE // 2
+            flat = jnp.swapaxes(raw[slot, part * half:(part + 1) * half], 0, 1)
+            for c in range(KV_HEADS):
+                tmp[side, c, part * half:(part + 1) * half, :] = flat[c]
+
+        @pl.when(i + RING < n)
+        def _():
+            pltpu.make_async_copy(src_ref.at[pl.ds((i + RING) * PIECE, PIECE)], raw.at[slot], sem.at[slot]).start()
+
+        put(i, side).start()
+        return carry
+
+    lax.fori_loop(0, n, piece, 0)
+    put(n - 2, 0).wait()
+    put(n - 1, 1).wait()
+
+
 def layer_kernel(resharded, a_ref, bias_ref, trig_ref, k4_ref, v4_ref, *refs):
     if resharded:
         kin_ref, vin_ref, wq_ref, wk_ref, wv_ref, wo_ref = refs[:6]
         refs = refs[6:]
     else:
-        wq_ref, wk_ref, wv_ref, wo_ref = refs[:4]
-        refs = refs[4:]
+        knext_ref, vnext_ref, wq_ref, wk_ref, wv_ref, wo_ref = refs[:6]
+        refs = refs[6:]
+        kpack_ref, vpack_ref = refs[3:5]
+        raw, tmp, raw_sem, out_sem = refs[-4:]
+        refs = refs[:3] + refs[5:-4]
     (y_ref, knew_ref, vnew_ref, xn, trig, wkv, wo, kb, vb, vt, msg, got, peer_new, newk, newv, qt,
-     s_even, s_odd, m_even, m_odd, acc, m_run, l_run, hide, o_send, o_all,
+     s_even, s_odd, m_even, m_odd, acc, m_run, l_run, hide, o_send, o_all, y_acc,
      trig_sem, w_sem, wo_sem, loc_sem, kv_send, kv_recv, pair_send, pair_recv, q_send, q_recv,
      new_send, new_recv, o_ssem, o_rsem) = refs
     chip, core, across, partner = peers()
@@ -183,6 +228,11 @@
         newk[s * tok:(s + 1) * tok, :] = parts[s][GROUP]
         newv[s * tok:(s + 1) * tok, :] = parts[s][GROUP + 1]
 
+    def relay(step):
+        for which in range(2):
+            kv_copy(step, which).wait_recv()
+            pair_copy(step, which).start()
+
     def ready(j):
         for jj in range(CHIPS):
             @pl.when(j == jj)
@@ -193,10 +243,8 @@
                 elif resharded:
                     for c in loads[2 * jj - 1]:
                         c.wait()
-                else:
-                    for which in range(2):
-                        kv_copy(jj, which).wait_recv()
-                        pair_copy(jj, which).start()
+                elif jj != 2:
+                    relay(jj)
         vt[j % 2, :, :chunk] = vb[2 * j].T
         for jj in range(CHIPS):
             @pl.when(j == jj)
@@ -274,6 +322,17 @@
     def step(item, carry):
         nxt = item + 1
 
+        if not resharded:
+            @pl.when(nxt == GROUP)
+            def _():
+                for src, dst in ((knext_ref, kpack_ref), (vnext_ref, vpack_ref)):
+                    pack_start(src, raw, raw_sem)
+                    pack_heads(src, dst, raw, tmp, raw_sem, out_sem)
+
+            @pl.when(nxt == GROUP + 4)
+            def _():
+                relay(2)
+
         @pl.when((nxt % GROUP == 0) & (nxt < n_items))
         def _():
             ready(nxt // GROUP)
@@ -307,19 +366,41 @@
 
     lax.fori_loop(0, n_items, step, 0)
     o_copies = [o_copy(g, s) for g in range(GROUP) for s in range(1, CHIPS)]
+    last = 3 * (GROUP - 1)
     wo_load.wait()
-    for c in o_copies:
+    for c in o_copies[:last]:
         c.wait_recv()
 
+    def heads(s, first, count):
+        at = pl.multiple_of((chip ^ s) * wide_cols + first * HEAD, HEAD)
+        return pl.ds(at, count * HEAD)
+
+    def early_proj(blk, carry):
+        cols = pl.ds(pl.multiple_of(blk * COL, COL), COL)
+        total = jnp.zeros((tok, COL), jnp.float32)
+        for s in range(CHIPS):
+            part = heads(s, 0, GROUP if s == 0 else GROUP - 1)
+            total = total + jnp.dot(o_all[:, part], wo[part, cols], preferred_element_type=jnp.float32)
+        y_acc[:, cols] = total
+        return carry
+
+    lax.fori_loop(0, wo.shape[1] // COL, early_proj, 0)
+    for c in o_copies[last:]:
+        c.wait_recv()
+
     def out_proj(blk, carry):
-        cols = pl.ds(pl.multiple_of(blk * COL, COL), COL)
-        y = jnp.dot(o_all[...], wo[:, cols], preferred_element_type=jnp.float32).astype(jnp.bfloat16)
+        cols = pl.ds(pl.multiple_of(blk * 2 * COL, 2 * COL), 2 * COL)
+        total = y_acc[:, cols]
+        for s in range(1, CHIPS):
+            part = heads(s, GROUP - 1, 1)
+            total = total + jnp.dot(o_all[:, part], wo[part, cols], preferred_element_type=jnp.float32)
+        y = total.astype(jnp.bfloat16)
         if not resharded:
             y = (a_ref[:, cols].astype(jnp.float32) + y.astype(jnp.float32)).astype(jnp.bfloat16)
         y_ref[:, cols] = y
         return carry
 
-    lax.fori_loop(0, wo.shape[1] // COL, out_proj, 0)
+    lax.fori_loop(0, wo.shape[1] // (2 * COL), out_proj, 0)
 
     for c in q_copies + new_copies + o_copies:
         c.wait_send()
@@ -331,8 +412,7 @@
                     kv_copy(step, which).wait_send()
 
 
-def run_layer(a, bias, trig, k4, v4, k_in, v_in, w_q, w_k, w_v, w_o, collective_id):
-    resharded = k_in is not None
+def run_layer(resharded, a, bias, trig, k4, v4, k_in, v_in, w_q, w_k, w_v, w_o, collective_id):
     tok, width = a.shape
     chunk = k4.shape[1]
     rows = CHIPS * tok
@@ -340,14 +420,19 @@
     vmem = pl.BlockSpec(memory_space=pltpu.VMEM)
     hbm = pl.BlockSpec(memory_space=pl.ANY)
     dma = pltpu.SemaphoreType.DMA
-    caches = (k4, v4, k_in, v_in) if resharded else (k4, v4)
+    packed = [] if resharded else [jax.ShapeDtypeStruct(k4.shape, bf16)] * 2
+    packing = [] if resharded else [
+        pltpu.VMEM((RING, PIECE, KV_HEADS, HEAD), bf16),
+        pltpu.VMEM((2, KV_HEADS, PIECE, HEAD), bf16),
+        dma((RING,)), dma((2,)),
+    ]
     return pl.pallas_call(
         functools.partial(layer_kernel, resharded),
         out_shape=[jax.ShapeDtypeStruct((tok, width), bf16),
                    jax.ShapeDtypeStruct((KV_HEADS, tok, HEAD), bf16),
-                   jax.ShapeDtypeStruct((KV_HEADS, tok, HEAD), bf16)],
-        in_specs=[vmem] * 2 + [hbm] * (len(caches) + 5),
-        out_specs=[vmem] * 3,
+                   jax.ShapeDtypeStruct((KV_HEADS, tok, HEAD), bf16)] + packed,
+        in_specs=[vmem] * 2 + [hbm] * 9,
+        out_specs=[vmem] * 3 + [hbm] * len(packed),
         scratch_shapes=[
             pltpu.VMEM((tok, width), bf16),
             pltpu.VMEM((tok, 2 * HEAD), f32),
@@ -372,14 +457,15 @@
             pltpu.VMEM((2 * rows, rows), f32),
             pltpu.VMEM((GROUP, CHIPS, tok, HEAD), bf16),
             pltpu.VMEM((tok, CHIPS * GROUP * HEAD), bf16),
+            pltpu.VMEM((tok, width), f32),
             dma, dma((2 + CHIPS,)), dma, dma((2 * SLOTS,)),
             dma((CHIPS - 1, 2)), dma((CHIPS - 1, 2)), dma((CHIPS, 2)), dma((CHIPS, 2)),
             dma((CHIPS - 1,)), dma((CHIPS - 1,)), dma((CHIPS,)), dma((CHIPS,)),
             dma((GROUP, CHIPS - 1)), dma((GROUP, CHIPS - 1)),
-        ],
-        compiler_params=pltpu.CompilerParams(collective_id=collective_id, has_side_effects=True, vmem_limit_bytes=60 * MIB),
+        ] + packing,
+        compiler_params=pltpu.CompilerParams(collective_id=collective_id, has_side_effects=True, vmem_limit_bytes=VMEM_ALL),
         name="layer",
-    )(a, bias, trig, *caches, w_q, w_k, w_v, w_o)
+    )(a, bias, trig, k4, v4, k_in, v_in, w_q, w_k, w_v, w_o)
 
 
 def mlp_kernel(h_ref, k4_ref, v4_ref, gate_ref, up_ref, down_ref, g_ref, kout_ref, vout_ref,
@@ -532,10 +618,9 @@
         trig = rope_table(axis_size * cache_k1.shape[0], n_tok)
         bias = jnp.concatenate([b_q1, b_k1, b_q2, b_k2]).reshape(1, -1)
         k4a, v4a = heads_first(cache_k1), heads_first(cache_v1)
-        k4b, v4b = heads_first(cache_k2), heads_first(cache_v2)
-        resid_h, k_one, v_one = run_layer(x_in, bias, trig, k4a, v4a, None, None, w_q1, w_k1, w_v1, w_o1, 1)
+        resid_h, k_one, v_one, k4b, v4b = run_layer(False, x_in, bias, trig, k4a, v4a, cache_k2, cache_v2, w_q1, w_k1, w_v1, w_o1, 1)
         hidden, k_in, v_in = run_mlp(resid_h, k4b, v4b, w_gate, w_up, w_down, 2)
-        y_two, k_two, v_two = run_layer(hidden, bias, trig, k4b, v4b, k_in, v_in, w_q2, w_k2, w_v2, w_o2, 3)
+        y_two, k_two, v_two = run_layer(True, hidden, bias, trig, k4b, v4b, k_in, v_in, w_q2, w_k2, w_v2, w_o2, 3)
         return order_outputs(hidden, y_two, k_one, v_one, k_two, v_two)
 
     return jax.shard_map(forward, mesh=mesh, in_specs=in_specs, out_specs=out_specs, check_vma=False)

time: 237 us -> 235 us (level)
  local copies, waits for them, and re-layouts: 9.34 us -> 5.41 us
  Pallas kernels: 225 us -> 228 us
    unnamed x10 -> x4, local copies, waits for them, and re-layouts: 8.71 us -> 4.78 us
    pallas_call x2, Pallas kernels: 156 us -> 159 us  [run_layer(): pl.pallas_call(functools.partial(layer_kernel, resharded), out_shape=[jax...]
where the time goes in v5:
time: 235 us
  Pallas kernels  228 us (97%)
  local copies, waits for them, and re-layouts  5.41 us (2%)
    pallas_call x2, Pallas kernels, run_layer(): pl.pallas_call(functools.partial(layer_kernel, resharded), out_shape=[jax...  159 us
    pallas_call x1, Pallas kernels, run_mlp(): pl.pallas_call(mlp_kernel, out_shape=[jax.ShapeDtypeStruct((tok, width),...  66.5 us
    unnamed x4, local copies, waits for them, and re-layouts  4.78 us

profile of v5, /device:TPU:0, one launch (start us, length us, event | category | flops | bytes accessed | tf_op | source)
XLA Modules:
  0.0 235.1 jit_solution(7250818197294627584)
XLA Ops:
  0.6 0.0 copy-start
  0.6 0.9 pad_maximum_fusion
  1.5 0.6 reshape.15.bias_ref
  2.2 3.2 %copy.32 = bf16[2048,4,128]{2,0,1:T(8,128)(2,1)} copy(bf16[2048,4,128]{2,1,0:T(4,128)(2,1)} %param.22) | data formatting | bytes 4194304 | tf_op args[1]
  5.4 0.0 copy-done
  5.4 1.6 copy.31
  7.0 88.1 %layer.2 = (bf16[64,3584]{1,0:T(8,128)(2,1)}, bf16[4,64,128]{2,1,0:T(8,128)(2,1)}, bf16[4,64,128]{2,1,0:T(8,128)(2,1)}, bf16[4,2048,128]{2,1,0:T(8,128)(2,1)}, bf16[4,2048,128]{2,1,0:T(8,128)(2,1)}) custom-call(bf16[64,3584]{1,0:T(8,128)(2,1)} %a_ref.1, bf16[1,8192]{1,0:T(2,128)(2,1)} %reshape.15.bias_ref, f32[512,256]{1,0:T(8,128)} %constant.2.clone.trig_ref, ...), custom_call_target="tpu_custom_call" | custom-call | tf_op jit(solution)/shard_map/layer/pallas_call | solution.py:429
  95.1 66.5 %mlp.1 = (bf16[64,3584]{1,0:T(8,128)(2,1)}, bf16[8,2048,128]{2,1,0:T(8,128)(2,1)}, bf16[8,2048,128]{2,1,0:T(8,128)(2,1)}) custom-call(bf16[64,3584]{1,0:T(8,128)(2,1)} %get-tuple-element.17.h_ref, bf16[4,2048,128]{2,1,0:T(8,128)(2,1)} %get-tuple-element.18.k4_ref, bf16[4,2048,128]{2,1,0:T(8,128)(2,1)} %get-tuple-element.19.v4_ref, ...), custom_call_target="tpu_custom_call" | custom-call | tf_op jit(solution)/shard_map/mlp/pallas_call | solution.py:564
  161.6 70.8 %layer.3 = (bf16[64,3584]{1,0:T(8,128)(2,1)}, bf16[4,64,128]{2,1,0:T(8,128)(2,1)}, bf16[4,64,128]{2,1,0:T(8,128)(2,1)}) custom-call(bf16[64,3584]{1,0:T(8,128)(2,1)} %get-tuple-element.20.a_ref.g_ref, bf16[1,8192]{1,0:T(2,128)(2,1)} %reshape.15.bias_ref, f32[512,256]{1,0:T(8,128)} %constant.2.clone.trig_ref, bf16[4,2048,128]{2,1,0:T(8,128)(2,1)} %get-tuple-element.18.k4_ref, ...), custom_call_target="tpu_custom_call" | custom-call | tf_op jit(solution)/shard_map/layer/pallas_call | solution.py:429
  232.4 2.7 %order_outputs.1 = (bf16[64,3584]{1,0:T(8,128)(2,1)}, bf16[64,3584]{1,0:T(8,128)(2,1)}, bf16[64,4,128]{2,1,0:T(4,128)(2,1)}, bf16[64,4,128]{2,1,0:T(4,128)(2,1)}...) custom-call(bf16[64,3584]{1,0:T(8,128)(2,1)} %get-tuple-element.20.a_ref.g_ref, ...), custom_call_target="tpu_custom_call" | custom-call | tf_op jit(solution)/shard_map/order_outputs/pallas_call | solution.py:602
Async XLA Ops:
  0.6 4.7 %copy-start = (bf16[2048,4,128]{2,1,0:T(4,128)(2,1)S(1)}, bf16[2048,4,128]{2,1,0:T(4,128)(2,1)}, u32[]{:S(2)}) copy-start(bf16[2048,4,128]{2,1,0:T(4,128)(2,1)} %param.23) | copy-start | bytes 6291460

commit v6 on v5

--- a/solution.py
+++ b/solution.py
@@ -109,7 +109,7 @@
     (y_ref, knew_ref, vnew_ref, xn, trig, wkv, wo, kb, vb, vt, msg, got, peer_new, newk, newv, qt,
      s_even, s_odd, m_even, m_odd, acc, m_run, l_run, hide, o_send, o_all, y_acc,
      trig_sem, w_sem, wo_sem, loc_sem, kv_send, kv_recv, pair_send, pair_recv, q_send, q_recv,
-     new_send, new_recv, o_ssem, o_rsem) = refs
+     new_send, new_recv, o_ssem, o_rsem, kvm_send, kvm_recv) = refs
     chip, core, across, partner = peers()
     me = 2 * chip + core
     scale2 = HEAD ** -0.5 * LOG2E
@@ -129,7 +129,7 @@
     kv_loads = [pltpu.make_async_copy(wk_ref, wkv.at[0], w_sem.at[0]), pltpu.make_async_copy(wv_ref, wkv.at[1], w_sem.at[1])]
     trig_load = pltpu.make_async_copy(trig_ref.at[pl.ds(me * tok, tok)], trig, trig_sem)
     trig_load.start()
-    for c in kv_loads + [wq_copy(n) for n in range(CHIPS)]:
+    for c in [wq_copy(n) for n in range(CHIPS)] + kv_loads:
         c.start()
     meet(across[1:] + [partner])
 
@@ -176,6 +176,27 @@
         wide = plain.astype(jnp.float32)
         return (wide * trig[:, :HEAD] + pltpu.roll(wide, HEAD // 2, 1) * trig[:, HEAD:]).astype(jnp.bfloat16)
 
+    def q_copy(n):
+        return remote(msg.at[n, pl.ds(0, GROUP)], got.at[n, pl.ds(0, GROUP)], q_send.at[n], q_recv.at[n],
+                      2 * (chip ^ (CHIPS - 1 - n)) + core)
+
+    def project(n, carry):
+        pltpu.make_async_copy(wo.at[:, :wide_cols], wo.at[:, :wide_cols], w_sem.at[2 + n]).wait()
+        grp = chip ^ (CHIPS - 1 - n)
+        cols = pl.ds(pl.multiple_of(n * wide_cols, HEAD), wide_cols)
+        bias = bias_ref[:, pl.ds(pl.multiple_of(bias_at + grp * wide_cols, HEAD), wide_cols)].astype(jnp.float32)
+        q_pre = (jnp.dot(xn[...], wo[:, cols], preferred_element_type=jnp.float32) + bias).astype(jnp.bfloat16)
+        for g in range(GROUP):
+            msg[n, g] = rope(q_pre[:, g * HEAD:(g + 1) * HEAD])
+        @pl.when(n < CHIPS - 1)
+        def _():
+            q_copy(n).start()
+
+        return carry
+
+    if not resharded:
+        pack_start(knext_ref, raw, raw_sem)
+    lax.fori_loop(0, CHIPS, project, 0)
     kv_loads[0].wait()
     k_pre = (jnp.dot(xn[...], wkv[0], preferred_element_type=jnp.float32)
              + bias_ref[:, bias_at + n_q:bias_at + n_q + KV_HEADS * HEAD].astype(jnp.float32)).astype(jnp.bfloat16)
@@ -186,33 +207,25 @@
     for c in range(KV_HEADS):
         vnew_ref[c] = v_pre[:, c * HEAD:(c + 1) * HEAD]
 
-    def q_copy(n):
-        return remote(msg.at[n], got.at[n], q_send.at[n], q_recv.at[n], 2 * (chip ^ (CHIPS - 1 - n)) + core)
-
-    def project(n, carry):
-        pltpu.make_async_copy(wo.at[:, :wide_cols], wo.at[:, :wide_cols], w_sem.at[2 + n]).wait()
+    kv_msgs = []
+    for n in range(CHIPS):
         grp = chip ^ (CHIPS - 1 - n)
-        cols = pl.ds(pl.multiple_of(n * wide_cols, HEAD), wide_cols)
-        bias = bias_ref[:, pl.ds(pl.multiple_of(bias_at + grp * wide_cols, HEAD), wide_cols)].astype(jnp.float32)
-        q_pre = (jnp.dot(xn[...], wo[:, cols], preferred_element_type=jnp.float32) + bias).astype(jnp.bfloat16)
-        for g in range(GROUP):
-            msg[n, g] = rope(q_pre[:, g * HEAD:(g + 1) * HEAD])
         msg[n, GROUP] = knew_ref[grp]
         msg[n, GROUP + 1] = vnew_ref[grp]
-
-        @pl.when(n < CHIPS - 1)
-        def _():
-            q_copy(n).start()
-
-        return carry
-
-    lax.fori_loop(0, CHIPS, project, 0)
+        if n < CHIPS - 1:
+            kv_msgs.append(remote(msg.at[n, pl.ds(GROUP, 2)], got.at[n, pl.ds(GROUP, 2)], kvm_send.at[n], kvm_recv.at[n],
+                                  2 * grp + core))
+            kv_msgs[-1].start()
     q_copies = [q_copy(n) for n in range(CHIPS - 1)]
     parts = [msg.at[CHIPS - 1]] + [got.at[CHIPS - 1 - s] for s in range(1, CHIPS)]
     wo_load = pltpu.make_async_copy(wo_ref, wo, wo_sem)
     if not resharded:
         for step, which in ((1, 1), (2, 1), (3, 0), (3, 1)):
             kv_copy(step, which).start()
+    if not resharded:
+        pack_heads(knext_ref, kpack_ref, raw, tmp, raw_sem, out_sem)
+        pack_start(vnext_ref, raw, raw_sem)
+        pack_heads(vnext_ref, vpack_ref, raw, tmp, raw_sem, out_sem)
     wo_load.start()
     acc[...] = jnp.zeros_like(acc)
     m_run[...] = jnp.full_like(m_run, -jnp.inf)
@@ -220,14 +233,8 @@
     for c in q_copies:
         c.wait_recv()
     new_copies = [remote(parts[s].at[pl.ds(GROUP, 2)], peer_new.at[s], new_send.at[s], new_recv.at[s], partner) for s in range(CHIPS)]
-    for c in new_copies:
-        c.start()
     for g in range(GROUP):
         qt[g] = jnp.concatenate([p[g] for p in parts], axis=0).T
-    for s in range(CHIPS):
-        newk[s * tok:(s + 1) * tok, :] = parts[s][GROUP]
-        newv[s * tok:(s + 1) * tok, :] = parts[s][GROUP + 1]
-
     def relay(step):
         for which in range(2):
             kv_copy(step, which).wait_recv()
@@ -323,12 +330,6 @@
         nxt = item + 1
 
         if not resharded:
-            @pl.when(nxt == GROUP)
-            def _():
-                for src, dst in ((knext_ref, kpack_ref), (vnext_ref, vpack_ref)):
-                    pack_start(src, raw, raw_sem)
-                    pack_heads(src, dst, raw, tmp, raw_sem, out_sem)
-
             @pl.when(nxt == GROUP + 4)
             def _():
                 relay(2)
@@ -336,6 +337,16 @@
         @pl.when((nxt % GROUP == 0) & (nxt < n_items))
         def _():
             ready(nxt // GROUP)
+
+        @pl.when(item == 2)
+        def _():
+            for c in kv_msgs:
+                c.wait_recv()
+            for c in new_copies:
+                c.start()
+            for s in range(CHIPS):
+                newk[s * tok:(s + 1) * tok, :] = parts[s][GROUP]
+                newv[s * tok:(s + 1) * tok, :] = parts[s][GROUP + 1]
 
         @pl.when(item == n_first)
         def _():
@@ -402,7 +413,7 @@
 
     lax.fori_loop(0, wo.shape[1] // (2 * COL), out_proj, 0)
 
-    for c in q_copies + new_copies + o_copies:
+    for c in q_copies + kv_msgs + new_copies + o_copies:
         c.wait_send()
     if not resharded:
         for step in range(CHIPS):
@@ -461,7 +472,7 @@
             dma, dma((2 + CHIPS,)), dma, dma((2 * SLOTS,)),
             dma((CHIPS - 1, 2)), dma((CHIPS - 1, 2)), dma((CHIPS, 2)), dma((CHIPS, 2)),
             dma((CHIPS - 1,)), dma((CHIPS - 1,)), dma((CHIPS,)), dma((CHIPS,)),
-            dma((GROUP, CHIPS - 1)), dma((GROUP, CHIPS - 1)),
+            dma((GROUP, CHIPS - 1)), dma((GROUP, CHIPS - 1)), dma((CHIPS - 1,)), dma((CHIPS - 1,)),
         ] + packing,
         compiler_params=pltpu.CompilerParams(collective_id=collective_id, has_side_effects=True, vmem_limit_bytes=VMEM_ALL),
         name="layer",

time: 235 us -> 228 us (0.970)
  Pallas kernels: 228 us -> 220 us
    pallas_call x2, Pallas kernels: 159 us -> 151 us  [run_layer(): pl.pallas_call(functools.partial(layer_kernel, resharded), out_shape=[jax...]
where the time goes in v6:
time: 228 us; the launch traced here: 227 us
  Pallas kernels  220 us (96%)
  local copies, waits for them, and re-layouts  5.41 us (2%)
    pallas_call x2, Pallas kernels, run_layer(): pl.pallas_call(functools.partial(layer_kernel, resharded), out_shape=[jax...  151 us
    pallas_call x1, Pallas kernels, run_mlp(): pl.pallas_call(mlp_kernel, out_shape=[jax.ShapeDtypeStruct((tok, width),...  66.6 us
    unnamed x4, local copies, waits for them, and re-layouts  4.78 us

profile of v6, /device:TPU:0, one launch (start us, length us, event | category | flops | bytes accessed | tf_op | source)
XLA Modules:
  0.0 227.3 jit_solution(7443977381622328097)
XLA Ops:
  0.6 0.0 copy-start
  0.6 0.9 pad_maximum_fusion
  1.5 0.6 reshape.15.bias_ref
  2.2 3.2 %copy.32 = bf16[2048,4,128]{2,0,1:T(8,128)(2,1)} copy(bf16[2048,4,128]{2,1,0:T(4,128)(2,1)} %param.22) | data formatting | bytes 4194304 | tf_op args[1]
  5.4 0.0 copy-done
  5.4 1.6 copy.31
  7.0 82.6 %layer.2 = (bf16[64,3584]{1,0:T(8,128)(2,1)}, bf16[4,64,128]{2,1,0:T(8,128)(2,1)}, bf16[4,64,128]{2,1,0:T(8,128)(2,1)}, bf16[4,2048,128]{2,1,0:T(8,128)(2,1)}, bf16[4,2048,128]{2,1,0:T(8,128)(2,1)}) custom-call(bf16[64,3584]{1,0:T(8,128)(2,1)} %a_ref.1, bf16[1,8192]{1,0:T(2,128)(2,1)} %reshape.15.bias_ref, f32[512,256]{1,0:T(8,128)} %constant.2.clone.trig_ref, ...), custom_call_target="tpu_custom_call" | custom-call | tf_op jit(solution)/shard_map/layer/pallas_call | solution.py:440
  89.6 66.6 %mlp.1 = (bf16[64,3584]{1,0:T(8,128)(2,1)}, bf16[8,2048,128]{2,1,0:T(8,128)(2,1)}, bf16[8,2048,128]{2,1,0:T(8,128)(2,1)}) custom-call(bf16[64,3584]{1,0:T(8,128)(2,1)} %get-tuple-element.17.h_ref, bf16[4,2048,128]{2,1,0:T(8,128)(2,1)} %get-tuple-element.18.k4_ref, bf16[4,2048,128]{2,1,0:T(8,128)(2,1)} %get-tuple-element.19.v4_ref, ...), custom_call_target="tpu_custom_call" | custom-call | tf_op jit(solution)/shard_map/mlp/pallas_call | solution.py:575
  156.3 68.4 %layer.3 = (bf16[64,3584]{1,0:T(8,128)(2,1)}, bf16[4,64,128]{2,1,0:T(8,128)(2,1)}, bf16[4,64,128]{2,1,0:T(8,128)(2,1)}) custom-call(bf16[64,3584]{1,0:T(8,128)(2,1)} %get-tuple-element.20.a_ref.g_ref, bf16[1,8192]{1,0:T(2,128)(2,1)} %reshape.15.bias_ref, f32[512,256]{1,0:T(8,128)} %constant.2.clone.trig_ref, bf16[4,2048,128]{2,1,0:T(8,128)(2,1)} %get-tuple-element.18.k4_ref, ...), custom_call_target="tpu_custom_call" | custom-call | tf_op jit(solution)/shard_map/layer/pallas_call | solution.py:440
  224.7 2.7 %order_outputs.1 = (bf16[64,3584]{1,0:T(8,128)(2,1)}, bf16[64,3584]{1,0:T(8,128)(2,1)}, bf16[64,4,128]{2,1,0:T(4,128)(2,1)}, bf16[64,4,128]{2,1,0:T(4,128)(2,1)}...) custom-call(bf16[64,3584]{1,0:T(8,128)(2,1)} %get-tuple-element.20.a_ref.g_ref, ...), custom_call_target="tpu_custom_call" | custom-call | tf_op jit(solution)/shard_map/order_outputs/pallas_call | solution.py:613
Async XLA Ops:
  0.6 4.7 %copy-start = (bf16[2048,4,128]{2,1,0:T(4,128)(2,1)S(1)}, bf16[2048,4,128]{2,1,0:T(4,128)(2,1)}, u32[]{:S(2)}) copy-start(bf16[2048,4,128]{2,1,0:T(4,128)(2,1)} %param.23) | copy-start | bytes 6291460

commit v7 on v6

--- a/solution.py
+++ b/solution.py
@@ -96,7 +96,7 @@
     put(n - 1, 1).wait()
 
 
-def layer_kernel(resharded, a_ref, bias_ref, trig_ref, k4_ref, v4_ref, *refs):
+def layer_kernel(resharded, a_ref, bq_ref, bk_ref, trig_ref, k4_ref, v4_ref, *refs):
     if resharded:
         kin_ref, vin_ref, wq_ref, wk_ref, wv_ref, wo_ref = refs[:6]
         refs = refs[6:]
@@ -109,7 +109,7 @@
     (y_ref, knew_ref, vnew_ref, xn, trig, wkv, wo, kb, vb, vt, msg, got, peer_new, newk, newv, qt,
      s_even, s_odd, m_even, m_odd, acc, m_run, l_run, hide, o_send, o_all, y_acc,
      trig_sem, w_sem, wo_sem, loc_sem, kv_send, kv_recv, pair_send, pair_recv, q_send, q_recv,
-     new_send, new_recv, o_ssem, o_rsem, kvm_send, kvm_recv) = refs
+     new_send, new_recv, o_ssem, o_rsem, kvm_send, kvm_recv, b_q, b_k) = refs
     chip, core, across, partner = peers()
     me = 2 * chip + core
     scale2 = HEAD ** -0.5 * LOG2E
@@ -117,10 +117,8 @@
     chunk = kb.shape[1]
     rows = qt.shape[2]
     wide_cols = GROUP * HEAD
-    n_q = wq_ref.shape[1]
     n_items = CHIPS * GROUP
     n_first = (CHIPS - 1) * GROUP
-    bias_at = (n_q + wk_ref.shape[1]) if resharded else 0
 
     def wq_copy(n):
         cols = pl.ds(pl.multiple_of((chip ^ (CHIPS - 1 - n)) * wide_cols, HEAD), wide_cols)
@@ -170,6 +168,8 @@
     else:
         xn[...] = a_ref[...]
 
+    b_q[...] = bq_ref[...].astype(jnp.float32)
+    b_k[...] = bk_ref[...].astype(jnp.float32)
     trig_load.wait()
 
     def rope(plain):
@@ -184,10 +184,10 @@
         pltpu.make_async_copy(wo.at[:, :wide_cols], wo.at[:, :wide_cols], w_sem.at[2 + n]).wait()
         grp = chip ^ (CHIPS - 1 - n)
         cols = pl.ds(pl.multiple_of(n * wide_cols, HEAD), wide_cols)
-        bias = bias_ref[:, pl.ds(pl.multiple_of(bias_at + grp * wide_cols, HEAD), wide_cols)].astype(jnp.float32)
-        q_pre = (jnp.dot(xn[...], wo[:, cols], preferred_element_type=jnp.float32) + bias).astype(jnp.bfloat16)
+        q_pre = jnp.dot(xn[...], wo[:, cols], preferred_element_type=jnp.float32)
         for g in range(GROUP):
-            msg[n, g] = rope(q_pre[:, g * HEAD:(g + 1) * HEAD])
+            row = b_q[pl.ds(grp * GROUP + g, 1), :]
+            msg[n, g] = rope((q_pre[:, g * HEAD:(g + 1) * HEAD] + row).astype(jnp.bfloat16))
         @pl.when(n < CHIPS - 1)
         def _():
             q_copy(n).start()
@@ -198,10 +198,9 @@
         pack_start(knext_ref, raw, raw_sem)
     lax.fori_loop(0, CHIPS, project, 0)
     kv_loads[0].wait()
-    k_pre = (jnp.dot(xn[...], wkv[0], preferred_element_type=jnp.float32)
-             + bias_ref[:, bias_at + n_q:bias_at + n_q + KV_HEADS * HEAD].astype(jnp.float32)).astype(jnp.bfloat16)
+    k_pre = jnp.dot(xn[...], wkv[0], preferred_element_type=jnp.float32)
     for c in range(KV_HEADS):
-        knew_ref[c] = rope(k_pre[:, c * HEAD:(c + 1) * HEAD])
+        knew_ref[c] = rope((k_pre[:, c * HEAD:(c + 1) * HEAD] + b_k[c:c + 1, :]).astype(jnp.bfloat16))
     kv_loads[1].wait()
     v_pre = jnp.dot(xn[...], wkv[1], preferred_element_type=jnp.float32).astype(jnp.bfloat16)
     for c in range(KV_HEADS):
@@ -423,7 +422,7 @@
                     kv_copy(step, which).wait_send()
 
 
-def run_layer(resharded, a, bias, trig, k4, v4, k_in, v_in, w_q, w_k, w_v, w_o, collective_id):
+def run_layer(resharded, a, b_q, b_k, trig, k4, v4, k_in, v_in, w_q, w_k, w_v, w_o, collective_id):
     tok, width = a.shape
     chunk = k4.shape[1]
     rows = CHIPS * tok
@@ -442,7 +441,7 @@
         out_shape=[jax.ShapeDtypeStruct((tok, width), bf16),
                    jax.ShapeDtypeStruct((KV_HEADS, tok, HEAD), bf16),
                    jax.ShapeDtypeStruct((KV_HEADS, tok, HEAD), bf16)] + packed,
-        in_specs=[vmem] * 2 + [hbm] * 9,
+        in_specs=[vmem] * 3 + [hbm] * 9,
         out_specs=[vmem] * 3 + [hbm] * len(packed),
         scratch_shapes=[
             pltpu.VMEM((tok, width), bf16),
@@ -473,10 +472,11 @@
             dma((CHIPS - 1, 2)), dma((CHIPS - 1, 2)), dma((CHIPS, 2)), dma((CHIPS, 2)),
             dma((CHIPS - 1,)), dma((CHIPS - 1,)), dma((CHIPS,)), dma((CHIPS,)),
             dma((GROUP, CHIPS - 1)), dma((GROUP, CHIPS - 1)), dma((CHIPS - 1,)), dma((CHIPS - 1,)),
+            pltpu.VMEM((w_q.shape[1] // HEAD, HEAD), f32), pltpu.VMEM((KV_HEADS, HEAD), f32),
         ] + packing,
         compiler_params=pltpu.CompilerParams(collective_id=collective_id, has_side_effects=True, vmem_limit_bytes=VMEM_ALL),
         name="layer",
-    )(a, bias, trig, k4, v4, k_in, v_in, w_q, w_k, w_v, w_o)
+    )(a, b_q.reshape(-1, HEAD), b_k.reshape(-1, HEAD), trig, k4, v4, k_in, v_in, w_q, w_k, w_v, w_o)
 
 
 def mlp_kernel(h_ref, k4_ref, v4_ref, gate_ref, up_ref, down_ref, g_ref, kout_ref, vout_ref,
@@ -627,11 +627,10 @@
     def forward(x_in, cache_k1, cache_v1, w_q1, b_q1, w_k1, b_k1, w_v1, w_o1, w_gate, w_up, w_down, cache_k2, cache_v2, w_q2, b_q2, w_k2, b_k2, w_v2, w_o2):
         n_tok = axis_size * x_in.shape[0]
         trig = rope_table(axis_size * cache_k1.shape[0], n_tok)
-        bias = jnp.concatenate([b_q1, b_k1, b_q2, b_k2]).reshape(1, -1)
         k4a, v4a = heads_first(cache_k1), heads_first(cache_v1)
-        resid_h, k_one, v_one, k4b, v4b = run_layer(False, x_in, bias, trig, k4a, v4a, cache_k2, cache_v2, w_q1, w_k1, w_v1, w_o1, 1)
+        resid_h, k_one, v_one, k4b, v4b = run_layer(False, x_in, b_q1, b_k1, trig, k4a, v4a, cache_k2, cache_v2, w_q1, w_k1, w_v1, w_o1, 1)
         hidden, k_in, v_in = run_mlp(resid_h, k4b, v4b, w_gate, w_up, w_down, 2)
-        y_two, k_two, v_two = run_layer(True, hidden, bias, trig, k4b, v4b, k_in, v_in, w_q2, w_k2, w_v2, w_o2, 3)
+        y_two, k_two, v_two = run_layer(True, hidden, b_q2, b_k2, trig, k4b, v4b, k_in, v_in, w_q2, w_k2, w_v2, w_o2, 3)
         return order_outputs(hidden, y_two, k_one, v_one, k_two, v_two)
 
     return jax.shard_map(forward, mesh=mesh, in_specs=in_specs, out_specs=out_specs, check_vma=False)

time: 228 us -> 226 us (level)
  no operation moved by 1% of the time
where the time goes in v7:
time: 226 us
  Pallas kernels  220 us (97%)
  local copies, waits for them, and re-layouts  4.93 us (2%)
    pallas_call x2, Pallas kernels, run_layer(): pl.pallas_call(functools.partial(layer_kernel, resharded), out_shape=[jax...  151 us
    pallas_call x1, Pallas kernels, run_mlp(): pl.pallas_call(mlp_kernel, out_shape=[jax.ShapeDtypeStruct((tok, width),...  66.6 us
    unnamed x4, local copies, waits for them, and re-layouts  4.93 us

profile of v7, /device:TPU:0, one launch (start us, length us, event | category | flops | bytes accessed | tf_op | source)
XLA Modules:
  0.0 226.0 jit_solution(15337505649107148084)
XLA Ops:
  0.6 0.0 copy-start
  0.6 3.3 %copy.32 = bf16[2048,4,128]{2,0,1:T(8,128)(2,1)} copy(bf16[2048,4,128]{2,1,0:T(4,128)(2,1)} %param.22) | data formatting | bytes 4194304 | tf_op args[1]
  4.0 0.0 copy-done
  4.0 1.6 copy.31
  5.6 82.7 %layer.2 = (bf16[64,3584]{1,0:T(8,128)(2,1)}, bf16[4,64,128]{2,1,0:T(8,128)(2,1)}, bf16[4,64,128]{2,1,0:T(8,128)(2,1)}, bf16[4,2048,128]{2,1,0:T(8,128)(2,1)}, bf16[4,2048,128]{2,1,0:T(8,128)(2,1)}) custom-call(bf16[64,3584]{1,0:T(8,128)(2,1)} %a_ref.1, bf16[28,128]{1,0:T(8,128)(2,1)} %bitcast.12, bf16[4,128]{1,0:T(4,128)(2,1)} %bitcast.14, ...), custom_call_target="tpu_custom_call" | custom-call | tf_op jit(solution)/shard_map/layer/pallas_call | solution.py:439
  88.3 66.6 %mlp.1 = (bf16[64,3584]{1,0:T(8,128)(2,1)}, bf16[8,2048,128]{2,1,0:T(8,128)(2,1)}, bf16[8,2048,128]{2,1,0:T(8,128)(2,1)}) custom-call(bf16[64,3584]{1,0:T(8,128)(2,1)} %get-tuple-element.17.h_ref, bf16[4,2048,128]{2,1,0:T(8,128)(2,1)} %get-tuple-element.18.k4_ref, bf16[4,2048,128]{2,1,0:T(8,128)(2,1)} %get-tuple-element.19.v4_ref, ...), custom_call_target="tpu_custom_call" | custom-call | tf_op jit(solution)/shard_map/mlp/pallas_call | solution.py:575
  154.9 68.4 %layer.3 = (bf16[64,3584]{1,0:T(8,128)(2,1)}, bf16[4,64,128]{2,1,0:T(8,128)(2,1)}, bf16[4,64,128]{2,1,0:T(8,128)(2,1)}) custom-call(bf16[64,3584]{1,0:T(8,128)(2,1)} %get-tuple-element.20.a_ref.g_ref, bf16[28,128]{1,0:T(8,128)(2,1)} %bitcast.13, bf16[4,128]{1,0:T(4,128)(2,1)} %bitcast.15, f32[512,256]{1,0:T(8,128)} %constant.2.clone.trig_ref, ...), custom_call_target="tpu_custom_call" | custom-call | tf_op jit(solution)/shard_map/layer/pallas_call | solution.py:439
  223.3 2.7 %order_outputs.1 = (bf16[64,3584]{1,0:T(8,128)(2,1)}, bf16[64,3584]{1,0:T(8,128)(2,1)}, bf16[64,4,128]{2,1,0:T(4,128)(2,1)}, bf16[64,4,128]{2,1,0:T(4,128)(2,1)}...) custom-call(bf16[64,3584]{1,0:T(8,128)(2,1)} %get-tuple-element.20.a_ref.g_ref, ...), custom_call_target="tpu_custom_call" | custom-call | tf_op jit(solution)/shard_map/order_outputs/pallas_call | solution.py:613
Async XLA Ops:
  0.6 3.4 %copy-start = (bf16[2048,4,128]{2,1,0:T(4,128)(2,1)S(1)}, bf16[2048,4,128]{2,1,0:T(4,128)(2,1)}, u32[]{:S(2)}) copy-start(bf16[2048,4,128]{2,1,0:T(4,128)(2,1)} %param.23) | copy-start | bytes 6291460
